TPU v7x, 32 devices: a whole 2x2x4 slice. The times are simulated.
32 devices in a mesh: seq: 8 (over y, x, core), head: 4 (over z).
Axes of the slice: x: 2, y: 2, z: 4, core: 2. Of those that a mesh axis runs over, the one named last changes fastest.
Arguments:
- queries: bfloat16 [16384, 512], P('seq', 'head'), may hold values from -6 to 6
- keys: bfloat16 [16384, 512], P('seq', 'head'), may hold values from -6 to 6
- values: bfloat16 [16384, 512], P('seq', 'head'), may hold values from -6 to 6
- level_ids: int32 [16384], P('seq'), may hold values from 0 to 63
- level_table: float32 [64, 15], replicated, may hold values from 0 to 4, as said below
- out_cotangent: bfloat16 [16384, 2048], P('seq', 'head'), may hold values from -6 to 6
Outputs:
- attn_out: bfloat16 [16384, 512], P('seq', 'head')
- weight_grad: float32 [2048, 512], P('seq', 'head')
Inputs may be any that keep to these rules, and one draw needn't show every extreme that they name: `level_table`: positive coefficients.
All inputs are finite; a program needn't handle non-finite values.
Results may differ from a plain program's by a relative error of at most 0.0043.
Values may be sent and summed in bfloat16 or wider, within the bound.
A program may use at most 64 MiB of HBM per device.

v0:
```python
import functools

import jax
import jax.numpy as jnp
from jax import lax
from jax.experimental import pallas as pl
from jax.experimental.pallas import tpu as pltpu
from jax.sharding import PartitionSpec as P

EPSILON = 1e-06
TILE = 128
CHUNKS = 8
KEEP = 5
MESH = pl.DeviceIdType.MESH
F32 = jnp.float32
BF16 = jnp.bfloat16


def dot(a, b, ca, cb):
    return lax.dot_general(a, b, (((ca,), (cb,)), ((), ())), preferred_element_type=F32)


def tile_levels(tile):
    row = lax.broadcasted_iota(jnp.int32, (tile, tile), 0)
    col = lax.broadcasted_iota(jnp.int32, (tile, tile), 1)
    apart = jnp.bitwise_xor(row, col)
    levels = jnp.zeros((tile, tile), jnp.int32)
    for bit in range(tile.bit_length() - 1):
        levels = levels + (jnp.right_shift(apart, bit) > 0).astype(jnp.int32)
    return jnp.where(col <= row, levels, -1)


def kernel(
    n_seq, n_head,
    q_hbm, k_hbm, v_hbm, ids_ref, table_ref, cot_hbm,
    attn_hbm, grad_ref,
    q_ref, k_ref, v_ref, cot_ref, levels_ref, coeff_ref, total_ref, sib_ref,
    state_ref, states_ref, flat_ref, attn_ref, gather_ref, acc_ref,
    share_ref, shares_ref, final_ref, finals_ref, help_ref,
    load_sem, out_sem, state_send, state_recv, ring_send, ring_recv,
    share_send, share_recv, final_send, final_recv, help_send, help_recv,
):
    seq, head = lax.axis_index("seq"), lax.axis_index("head")
    block_len, head_dim = q_ref.shape
    width = cot_ref.shape[1]
    tiles = block_len // TILE
    chunk = block_len // CHUNKS
    tile_bits = TILE.bit_length() - 1
    local_bits = block_len.bit_length() - 1
    inner = local_bits - tile_bits
    seq_bits = n_seq.bit_length() - 1
    owners = n_seq // n_head
    rows_per = max(16, head_dim // n_seq)
    reducers = head_dim // rows_per
    piece = finals_ref.shape[2]
    last = n_head - 1
    keep = CHUNKS - help_ref.shape[0] if n_head >= 4 else CHUNKS
    scale = (block_len * n_seq) ** (-0.5)

    loads = [
        pltpu.make_async_copy(src, dst, load_sem.at[i])
        for i, (src, dst) in enumerate(
            [(k_hbm, k_ref), (v_hbm, v_ref), (q_hbm, q_ref), (cot_hbm, cot_ref)]
        )
    ]
    for load in loads:
        load.start()

    barrier = pltpu.get_barrier_semaphore()
    me = seq * n_head + head

    def greet(step, carry):
        other = lax.rem(me + step, n_seq * n_head)
        pl.semaphore_signal(
            barrier, inc=1, device_id=(other // n_head, lax.rem(other, n_head)),
            device_id_type=MESH,
        )
        return carry

    lax.fori_loop(1, n_seq * n_head, greet, 0)

    table = table_ref[...]
    high = table.astype(BF16)
    rest = table - high.astype(F32)
    mid = rest.astype(BF16)
    low = (rest - mid.astype(F32)).astype(BF16)
    table3 = jnp.concatenate([high, mid, low], axis=1)
    levels_ref[...] = tile_levels(TILE)

    loads[0].wait()
    loads[1].wait()
    nodes = [
        dot(k_ref[pl.ds(i * TILE, TILE), :], v_ref[pl.ds(i * TILE, TILE), :], 0, 0)
        for i in range(tiles)
    ]
    for bit in range(inner):
        for i in range(tiles):
            place = (i >> bit) ^ 1
            value = nodes[place].astype(BF16) if (i >> bit) & 1 else jnp.zeros((head_dim, head_dim), BF16)
            sib_ref[i, :, pl.ds(bit * head_dim, head_dim)] = value
        nodes = [nodes[2 * i] + nodes[2 * i + 1] for i in range(len(nodes) // 2)]
    state_ref[...] = nodes[0].astype(BF16)

    pl.semaphore_wait(barrier, n_seq * n_head - 1)

    def state_copy(target):
        return pltpu.make_async_remote_copy(
            src_ref=state_ref, dst_ref=states_ref.at[seq],
            send_sem=state_send.at[target], recv_sem=state_recv.at[seq],
            device_id=(target, head), device_id_type=MESH,
        )

    for target in range(1, n_seq):
        @pl.when(seq < target)
        def _():
            state_copy(target).start()

    right, left = lax.rem(head + 1, n_head), lax.rem(head + n_head - 1, n_head)
    places = (head, last - head)

    def limit(c):
        return jnp.where(c < keep, last, last - 1)

    def help_copy(way, c):
        return pltpu.make_async_remote_copy(
            src_ref=cot_hbm.at[pl.ds(c * chunk, chunk), :], dst_ref=help_ref.at[c - keep],
            send_sem=help_send.at[c - keep], recv_sem=help_recv.at[c - keep],
            device_id=(seq, left if way == 0 else right), device_id_type=MESH,
        )

    for way in range(2):
        @pl.when(places[way] == last)
        def _():
            for c in range(keep, CHUNKS):
                help_copy(way, c).start()

    acc_ref[...] = jnp.zeros_like(acc_ref)

    loads[2].wait()

    def local_tile(i, carry):
        rows = pl.ds(pl.multiple_of(i * TILE, TILE), TILE)
        row_ids = lax.broadcasted_iota(jnp.int32, (table.shape[1], TILE), 0)
        onehot = (row_ids == ids_ref[:, rows]).astype(F32).astype(BF16)
        coeff = dot(jnp.concatenate([onehot] * 3, axis=0), table3, 0, 1)
        coeff_ref[rows, :] = coeff
        levels = levels_ref[...]
        weights = jnp.zeros((TILE, TILE), F32)
        for level in range(tile_bits + 1):
            weights = jnp.where(levels == level, coeff[:, level : level + 1], weights)
        query = q_ref[rows, :]
        scores = dot(query, k_ref[rows, :], 1, 1)
        total = dot((weights * scores).astype(BF16), v_ref[rows, :], 1, 0)
        readout = dot(query, sib_ref[i], 1, 0)
        for bit in range(inner):
            level = tile_bits + 1 + bit
            total += coeff[:, level : level + 1] * readout[:, bit * head_dim : (bit + 1) * head_dim]
        total_ref[rows, :] = total
        return carry

    lax.fori_loop(0, tiles, local_tile, 0, unroll=4)

    for bit in range(seq_bits):
        span = 2**bit
        node = seq // span
        columns = pl.ds(bit * head_dim, head_dim)

        @pl.when(lax.rem(node, 2) == 1)
        def _():
            total = jnp.zeros((head_dim, head_dim), F32)
            for offset in range(span):
                source = (node - 1) * span + offset
                pltpu.make_async_remote_copy(
                    src_ref=state_ref, dst_ref=states_ref.at[source],
                    send_sem=state_send.at[0], recv_sem=state_recv.at[source],
                    device_id=(source, head), device_id_type=MESH,
                ).wait_recv()
                total += states_ref[source].astype(F32)
            upper = total.astype(BF16)
            flat_ref[pl.ds(0, head_dim), columns] = upper
            flat_ref[pl.ds(head_dim, head_dim), columns] = (total - upper.astype(F32)).astype(BF16)

        @pl.when(lax.rem(node, 2) == 0)
        def _():
            flat_ref[:, columns] = jnp.zeros((2 * head_dim, head_dim), BF16)

    def origin_of(way, distance):
        return lax.rem(head + (n_head - distance if way == 0 else distance), n_head)

    def ring_copy(way, distance, c):
        origin = origin_of(way, distance)
        return pltpu.make_async_remote_copy(
            src_ref=gather_ref.at[origin, c], dst_ref=gather_ref.at[origin, c],
            send_sem=ring_send.at[way, distance, c], recv_sem=ring_recv.at[way, distance, c],
            device_id=(seq, right if way == 0 else left), device_id_type=MESH,
        )

    def ring_arrival(way, distance, c):
        origin = origin_of(way, distance)
        return pltpu.make_async_remote_copy(
            src_ref=gather_ref.at[origin, c], dst_ref=gather_ref.at[origin, c],
            send_sem=ring_send.at[way, distance - 1, c], recv_sem=ring_recv.at[way, distance - 1, c],
            device_id=(seq, right if way == 0 else left), device_id_type=MESH,
        )

    def attn_tile(first):
        def one(i, carry):
            rows = pl.ds(pl.multiple_of(first * chunk + i * TILE, TILE), TILE)
            query = q_ref[rows, :]
            readout = dot(jnp.concatenate([query, query], axis=1), flat_ref[...], 1, 0)
            coeff = coeff_ref[rows, :]
            cross = jnp.zeros((TILE, head_dim), F32)
            for bit in range(seq_bits):
                level = local_bits + 1 + bit
                cross += coeff[:, level : level + 1] * readout[:, bit * head_dim : (bit + 1) * head_dim]
            total = total_ref[rows, :] + cross
            normed = total * lax.rsqrt(jnp.mean(total * total, axis=1, keepdims=True) + EPSILON)
            attn_ref[rows, :] = normed.astype(BF16)
            gather_ref[head, first, :, pl.ds(pl.multiple_of(i * TILE, TILE), TILE)] = normed.T.astype(BF16)
            return carry
        return one

    for c in range(CHUNKS):
        lax.fori_loop(0, chunk // TILE, attn_tile(c), 0, unroll=True)
        for way in range(2):
            @pl.when(places[way] + 1 <= limit(c))
            def _():
                ring_copy(way, 0, c).start()

    attn_copy = pltpu.make_async_copy(attn_ref, attn_hbm, out_sem.at[0])
    attn_copy.start()

    def multiply(origin, c):
        rows = pl.ds(pl.multiple_of(c * chunk, chunk), chunk)
        acc_ref[origin] += dot(gather_ref[origin, c], cot_ref[rows, :], 1, 0)

    def multiply_help(origin, c):
        acc_ref[n_head + origin] += dot(gather_ref[origin, c], help_ref[c - keep], 1, 0)

    def share_copy(origin, target):
        return pltpu.make_async_remote_copy(
            src_ref=share_ref.at[origin, pl.ds(target * rows_per, rows_per), :],
            dst_ref=shares_ref.at[origin, seq],
            send_sem=share_send.at[origin, target], recv_sem=share_recv.at[origin, seq],
            device_id=(target, head), device_id_type=MESH,
        )

    def send_share(origin):
        share_ref[origin] = (acc_ref[origin] * scale).astype(BF16)
        for target in range(reducers):
            @pl.when(seq != target)
            def _():
                share_copy(origin, target).start()

    def final_copy(slot, block, origin, kind, owner):
        columns = pl.ds(owner * piece if piece < width else 0, piece)
        return pltpu.make_async_remote_copy(
            src_ref=final_ref.at[slot, :, columns] if piece < width else final_ref.at[slot],
            dst_ref=finals_ref.at[kind, pl.ds(pl.multiple_of(seq * rows_per, rows_per), rows_per), :],
            send_sem=final_send.at[slot, owner], recv_sem=final_recv.at[kind, seq],
            device_id=(block * owners + owner, origin), device_id_type=MESH,
        )

    def is_self(block, origin, owner):
        return jnp.logical_and(block * owners + owner == seq, origin == head)

    def reduce_share(slot, block, origin, kind):
        @pl.when(seq < reducers)
        def _():
            mine = pl.ds(pl.multiple_of(seq * rows_per, rows_per), rows_per)
            final_ref[slot] = acc_ref[slot, mine, :] * scale

            def add(step, carry):
                source = lax.rem(seq + step, n_seq)
                pltpu.make_async_remote_copy(
                    src_ref=share_ref.at[slot, pl.ds(0, rows_per), :],
                    dst_ref=shares_ref.at[slot, source],
                    send_sem=share_send.at[slot, 0], recv_sem=share_recv.at[slot, source],
                    device_id=(source, head), device_id_type=MESH,
                ).wait_recv()
                final_ref[slot] += shares_ref[slot, source].astype(F32)
                return carry

            lax.fori_loop(1, n_seq, add, 0)
            for owner in range(owners):
                @pl.when(jnp.logical_not(is_self(block, origin, owner)))
                def _():
                    final_copy(slot, block, origin, kind, owner).start()

                @pl.when(is_self(block, origin, owner))
                def _():
                    whole = final_ref[slot]
                    start = owner * piece if piece < width else 0
                    finals_ref[kind, mine, :] = whole[:, start : start + piece]

    loads[3].wait()

    def own_chunk(c, carry):
        multiply(head, c)
        return carry

    lax.fori_loop(0, CHUNKS, own_chunk, 0)
    send_share(head)
    every = [(head >= 0, head, head, head, 0)]
    waiting = list(every)
    helps = n_head >= 4
    for distance in range(1, n_head):
        def arrivals(c, carry):
            for way in range(2):
                place = places[way]

                @pl.when(jnp.logical_and(place >= distance, place <= limit(c)))
                def _():
                    ring_arrival(way, distance, c).wait_recv()
                    if distance < last:
                        @pl.when(place + 1 <= limit(c))
                        def _():
                            ring_copy(way, distance, c).start()
                    origin = origin_of(way, distance)
                    multiply(origin, c)
                    if helps and distance < last:
                        @pl.when(jnp.logical_and(place == last - 1, c >= keep))
                        def _():
                            if distance == 1:
                                help_copy(way, c).wait_recv()
                                multiply_help(head, c)
                            multiply_help(origin, c)
            return carry

        lax.fori_loop(0, CHUNKS, arrivals, 0)
        done = []
        for way in range(2):
            origin, place = origin_of(way, distance), places[way]
            done.append((place >= distance, origin, head, origin, 0))
            if helps and distance < last:
                block = last if way == 0 else 0
                helper = place == last - 1
                if distance == 1:
                    done.append((helper, n_head + head, block, head, 1))
                done.append((helper, n_head + origin, block, origin, 1))
        for condition, slot, _, _, _ in done:
            pl.when(condition)(functools.partial(send_share, slot))
        for condition, *rest in waiting:
            pl.when(condition)(functools.partial(reduce_share, *rest))
        every += done
        waiting = done
    for condition, *rest in waiting:
        pl.when(condition)(functools.partial(reduce_share, *rest))

    home = seq // owners
    at_end = jnp.logical_and(jnp.logical_or(home == 0, home == last), head != home)
    for kind in range(2 if helps else 1):
        plane = home if kind == 0 else jnp.where(home == 0, 1, last - 1)
        for source in range(reducers):
            away = jnp.logical_not(jnp.logical_and(seq == source, head == plane))

            @pl.when(jnp.logical_and(away, at_end) if kind else away)
            def _():
                pltpu.make_async_remote_copy(
                    src_ref=final_ref.at[0, :, pl.ds(0, piece)] if piece < width else final_ref.at[0],
                    dst_ref=finals_ref.at[kind, pl.ds(source * rows_per, rows_per), :],
                    send_sem=final_send.at[0, 0], recv_sem=final_recv.at[kind, source],
                    device_id=(source, plane), device_id_type=MESH,
                ).wait_recv()
    if helps:
        @pl.when(at_end)
        def _():
            finals_ref[0] += finals_ref[1]
    per = grad_ref.shape[1]
    if per == piece:
        grad_ref[...] = finals_ref[0]
    else:
        for owner in range(owners):
            @pl.when(lax.rem(seq, owners) == owner)
            def _():
                grad_ref[...] = finals_ref[0][:, owner * per : (owner + 1) * per]

    for target in range(1, n_seq):
        @pl.when(seq < target)
        def _():
            state_copy(target).wait_send()
    for way in range(2):
        place = places[way]

        @pl.when(place == last)
        def _():
            for c in range(keep, CHUNKS):
                help_copy(way, c).wait_send()

        for distance in range(last):
            def drain(c, carry):
                @pl.when(jnp.logical_and(place >= distance, place + 1 <= limit(c)))
                def _():
                    ring_copy(way, distance, c).wait_send()
                return carry

            lax.fori_loop(0, CHUNKS, drain, 0)
    for condition, slot, block, origin, kind in every:
        @pl.when(condition)
        def _():
            for target in range(reducers):
                @pl.when(seq != target)
                def _():
                    share_copy(slot, target).wait_send()

            @pl.when(seq < reducers)
            def _():
                for owner in range(owners):
                    @pl.when(jnp.logical_not(is_self(block, origin, owner)))
                    def _():
                        final_copy(slot, block, origin, kind, owner).wait_send()
    attn_copy.wait()


def body(n_seq, n_head, queries, keys, values, level_ids, level_table, out_cotangent):
    block_len, head_dim = queries.shape
    width = out_cotangent.shape[1]
    per = width * n_head // n_seq
    piece = per if per % 128 == 0 else width
    seq_bits = n_seq.bit_length() - 1
    inner = (block_len // TILE).bit_length() - 1
    rows_per = max(16, head_dim // n_seq)
    reducers = head_dim // rows_per
    steps = max(1, n_head - 1)
    slots = 2 * n_head
    dma = pltpu.SemaphoreType.DMA
    vmem = pl.BlockSpec(memory_space=pltpu.VMEM)
    hbm = pl.BlockSpec(memory_space=pl.ANY)
    attn_out, grad = pl.pallas_call(
        functools.partial(kernel, n_seq, n_head),
        out_shape=(
            jax.ShapeDtypeStruct((block_len, head_dim), BF16),
            jax.ShapeDtypeStruct((head_dim, per), F32),
        ),
        in_specs=[hbm, hbm, hbm, vmem, vmem, hbm],
        out_specs=(hbm, vmem),
        scratch_shapes=[
            pltpu.VMEM((block_len, head_dim), BF16),
            pltpu.VMEM((block_len, head_dim), BF16),
            pltpu.VMEM((block_len, head_dim), BF16),
            pltpu.VMEM((block_len, width), BF16),
            pltpu.VMEM((TILE, TILE), jnp.int32),
            pltpu.VMEM((block_len, level_table.shape[1]), F32),
            pltpu.VMEM((block_len, head_dim), F32),
            pltpu.VMEM((block_len // TILE, head_dim, inner * head_dim), BF16),
            pltpu.VMEM((head_dim, head_dim), BF16),
            pltpu.VMEM((n_seq, head_dim, head_dim), BF16),
            pltpu.VMEM((2 * head_dim, seq_bits * head_dim), BF16),
            pltpu.VMEM((block_len, head_dim), BF16),
            pltpu.VMEM((n_head, CHUNKS, head_dim, block_len // CHUNKS), BF16),
            pltpu.VMEM((slots, head_dim, width), F32),
            pltpu.VMEM((slots, head_dim, width), BF16),
            pltpu.VMEM((slots, n_seq, rows_per, width), BF16),
            pltpu.VMEM((slots, rows_per, width), F32),
            pltpu.VMEM((2, head_dim, piece), F32),
            pltpu.VMEM((CHUNKS - KEEP, block_len // CHUNKS, width), BF16),
            dma((4,)),
            dma((1,)),
            dma((n_seq,)),
            dma((n_seq,)),
            dma((2, steps, CHUNKS)),
            dma((2, steps, CHUNKS)),
            dma((slots, reducers)),
            dma((slots, n_seq)),
            dma((slots, n_seq // n_head)),
            dma((2, reducers)),
            dma((CHUNKS - KEEP,)),
            dma((CHUNKS - KEEP,)),
        ],
        compiler_params=pltpu.CompilerParams(
            collective_id=0, has_side_effects=True, vmem_limit_bytes=60 * 2**20
        ),
    )(queries, keys, values, level_ids[None, :], level_table.T, out_cotangent)
    return attn_out, grad.T


def solution(mesh):
    in_specs = (
        P("seq", "head"),
        P("seq", "head"),
        P("seq", "head"),
        P("seq"),
        P(),
        P("seq", "head"),
    )
    out_specs = (P("seq", "head"), P("seq", "head"))
    return jax.shard_map(
        functools.partial(body, mesh.shape["seq"], mesh.shape["head"]),
        mesh=mesh, in_specs=in_specs, out_specs=out_specs, check_vma=False,
    )
```

profile of v0, /device:TPU:25, one launch (start us, length us, event | category | flops | bytes accessed | tf_op | source)
XLA Modules:
  0.0 62.2 jit_solution(14245332560567421234)
XLA Ops:
  0.6 58.1 %shard_map.77 = (bf16[2048,128]{1,0:T(8,128)(2,1)}, f32[128,256]{1,0:T(8,128)}) custom-call(bf16[2048,128]{1,0:T(8,128)(2,1)} %q_hbm.1, bf16[2048,128]{1,0:T(8,128)(2,1)} %k_hbm.1, bf16[2048,128]{1,0:T(8,128)(2,1)} %v_hbm.1, s32[1,2048]{1,0:T(1,128)} %bitcast.4, f32[15,64]{1,0:T(8,128)} %bitcast.5, bf16[2048,512]{1,0:T(8,128)(2,1)} %cot_hbm.1), custom_call_target="tpu_custom_call" | custom-call | tf_op jit(solution)/shard_map/pallas_call | solution.py:429
  58.7 1.7 %copy.8 = f32[256,128]{1,0:T(8,128)} copy(f32[256,128]{0,1:T(8,128)} %bitcast.3) | data formatting | bytes 262144
  60.4 1.9 %copy.10 = bf16[2048,128]{1,0:T(8,128)(2,1)} copy(bf16[2048,128]{1,0:T(8,128)(2,1)} %get-tuple-element.10) | data formatting | bytes 1048576
where the time goes:
time: 62.5 us; the launch traced here: 62.2 us
  Pallas kernels  58.1 us (93%)
  local copies, waits for them, and re-layouts  3.53 us (6%)
  between operations  0.64 us (1%)
    pallas_call x1, Pallas kernels, body(): pl.pallas_call(functools.partial(kernel, n_seq, n_head), out_shape=(jax.S...  58.1 us
    unnamed x2, local copies, waits for them, and re-layouts  3.53 us

commit v1 on v0

v1 whole, which is shorter than its diff:
```python
import functools

import jax
import jax.numpy as jnp
from jax import lax
from jax.experimental import pallas as pl
from jax.experimental.pallas import tpu as pltpu
from jax.sharding import PartitionSpec as P

EPSILON = 1e-06
TILE = 128
KEEP = 12
FIRST = 6
FILL = 8
EARLY = 2
AHEAD = 7
LAG = 4
MESH = pl.DeviceIdType.MESH
F32 = jnp.float32
BF16 = jnp.bfloat16


def dot(a, b, ca, cb):
    return lax.dot_general(a, b, (((ca,), (cb,)), ((), ())), preferred_element_type=F32)


def tile_levels(tile):
    row = lax.broadcasted_iota(jnp.int32, (tile, tile), 0)
    col = lax.broadcasted_iota(jnp.int32, (tile, tile), 1)
    apart = jnp.bitwise_xor(row, col)
    levels = jnp.zeros((tile, tile), jnp.int32)
    for bit in range(tile.bit_length() - 1):
        levels = levels + (jnp.right_shift(apart, bit) > 0).astype(jnp.int32)
    return jnp.where(col <= row, levels, -1)


def kept_tiles(n_head, tiles):
    return tiles * KEEP // 16 if n_head >= 4 else tiles


def kernel(
    n_seq, n_head,
    q_hbm, k_hbm, v_hbm, ids_ref, table_ref, cot_hbm,
    attn_hbm, grad_ref,
    q_ref, k_ref, v_ref, cot_ref, levels_ref, coeff_ref, total_ref, sib_ref,
    state_ref, states_ref, flat_ref, attn_ref, gather_ref, acc_ref,
    share_ref, shares_ref, final_ref, finals_ref, help_ref,
    load_sem, out_sem, state_send, state_recv, ring_send, ring_recv,
    share_send, share_recv, final_send, final_recv, help_send, help_recv,
):
    seq, head = lax.axis_index("seq"), lax.axis_index("head")
    block_len, head_dim = q_ref.shape
    width = cot_ref.shape[1]
    tiles = block_len // TILE
    pairs = tiles // 2
    tile_bits = TILE.bit_length() - 1
    local_bits = block_len.bit_length() - 1
    inner = local_bits - tile_bits
    seq_bits = n_seq.bit_length() - 1
    owners = n_seq // n_head
    rows_per = max(16, head_dim // n_seq)
    reducers = head_dim // rows_per
    piece = finals_ref.shape[2]
    last = n_head - 1
    keep = kept_tiles(n_head, tiles)
    helps = keep < tiles
    first, fill = min(FIRST, keep), min(FILL, keep)
    quads = tiles // 4
    early = min(EARLY, tiles)
    ahead = min(AHEAD, tiles)
    scale = (block_len * n_seq) ** (-0.5)

    loads = [
        pltpu.make_async_copy(src, dst, load_sem.at[i])
        for i, (src, dst) in enumerate(
            [(k_hbm, k_ref), (v_hbm, v_ref), (q_hbm, q_ref), (cot_hbm, cot_ref)]
        )
    ]
    for load in loads:
        load.start()

    barrier = pltpu.get_barrier_semaphore()
    me = seq * n_head + head

    def greet(step, carry):
        other = lax.rem(me + step, n_seq * n_head)
        pl.semaphore_signal(
            barrier, inc=1, device_id=(other // n_head, lax.rem(other, n_head)),
            device_id_type=MESH,
        )
        return carry

    lax.fori_loop(1, n_seq * n_head, greet, 0)

    table = table_ref[...]
    high = table.astype(BF16)
    rest = table - high.astype(F32)
    mid = rest.astype(BF16)
    low = (rest - mid.astype(F32)).astype(BF16)
    table3 = jnp.concatenate([high, mid, low], axis=1)
    levels_ref[...] = tile_levels(TILE)

    loads[0].wait()
    loads[1].wait()
    nodes = [
        dot(k_ref[pl.ds(i * TILE, TILE), :], v_ref[pl.ds(i * TILE, TILE), :], 0, 0)
        for i in range(tiles)
    ]
    for bit in range(inner):
        for i in range(tiles):
            place = (i >> bit) ^ 1
            value = nodes[place].astype(BF16) if (i >> bit) & 1 else jnp.zeros((head_dim, head_dim), BF16)
            sib_ref[i, :, pl.ds(bit * head_dim, head_dim)] = value
        nodes = [nodes[2 * i] + nodes[2 * i + 1] for i in range(len(nodes) // 2)]
    state_ref[...] = nodes[0].astype(BF16)

    loads[2].wait()

    def local_tile(i):
        rows = pl.ds(pl.multiple_of(i * TILE, TILE), TILE)
        row_ids = lax.broadcasted_iota(jnp.int32, (table.shape[1], TILE), 0)
        onehot = (row_ids == ids_ref[:, rows]).astype(F32).astype(BF16)
        coeff = dot(jnp.concatenate([onehot] * 3, axis=0), table3, 0, 1)
        coeff_ref[rows, :] = coeff
        levels = levels_ref[...]
        weights = jnp.zeros((TILE, TILE), F32)
        for level in range(tile_bits + 1):
            weights = jnp.where(levels == level, coeff[:, level : level + 1], weights)
        query = q_ref[rows, :]
        scores = dot(query, k_ref[rows, :], 1, 1)
        total = dot((weights * scores).astype(BF16), v_ref[rows, :], 1, 0)
        readout = dot(query, sib_ref[i], 1, 0)
        for bit in range(inner):
            level = tile_bits + 1 + bit
            total += coeff[:, level : level + 1] * readout[:, bit * head_dim : (bit + 1) * head_dim]
        total_ref[rows, :] = total

    def local_tiles(start, stop):
        def one(i, carry):
            local_tile(i)
            return carry

        lax.fori_loop(start, stop, one, 0, unroll=True)

    with jax.named_scope("local0"):
        local_tiles(0, early)

    with jax.named_scope("barrier"):
        pl.semaphore_wait(barrier, n_seq * n_head - 1)

    def state_copy(target):
        return pltpu.make_async_remote_copy(
            src_ref=state_ref, dst_ref=states_ref.at[seq],
            send_sem=state_send.at[0], recv_sem=state_recv.at[0],
            device_id=(target, head), device_id_type=MESH,
        )

    for target in range(1, n_seq):
        @pl.when(seq < target)
        def _():
            state_copy(target).start()

    right, left = lax.rem(head + 1, n_head), lax.rem(head + n_head - 1, n_head)
    neighbours = (right, left)
    places = (head, last - head)

    def origin_of(way, step):
        return step if way == 0 else last - step

    def help_copy(way, c):
        return pltpu.make_async_remote_copy(
            src_ref=cot_hbm.at[pl.ds(c * TILE, TILE), :],
            dst_ref=help_ref.at[pl.ds((c - keep) * TILE, TILE), :],
            send_sem=help_send.at[0], recv_sem=help_recv.at[c - keep],
            device_id=(seq, left if way == 0 else right), device_id_type=MESH,
        )

    def start_helps(begin, end):
        for way in range(2):
            @pl.when(places[way] == last)
            def _():
                for c in range(begin, end):
                    help_copy(way, c).start()

    if helps:
        start_helps(keep, keep + 1)

    with jax.named_scope("local1"):
        local_tiles(early, ahead)
    acc_ref[...] = jnp.zeros_like(acc_ref)

    with jax.named_scope("states"):
        for block in range(1, n_seq):
            @pl.when(seq == block)
            def _():
                arrived = states_ref.at[pl.ds(0, block)]
                pltpu.make_async_remote_copy(
                    src_ref=arrived, dst_ref=arrived,
                    send_sem=state_send.at[0], recv_sem=state_recv.at[0],
                    device_id=(0, head), device_id_type=MESH,
                ).wait_recv()

    for bit in range(seq_bits):
        span = 2**bit
        node = seq // span
        columns = pl.ds(bit * head_dim, head_dim)

        @pl.when(lax.rem(node, 2) == 1)
        def _():
            total = jnp.zeros((head_dim, head_dim), F32)
            for offset in range(span):
                total += states_ref[(node - 1) * span + offset].astype(F32)
            upper = total.astype(BF16)
            flat_ref[pl.ds(0, head_dim), columns] = upper
            flat_ref[pl.ds(head_dim, head_dim), columns] = (total - upper.astype(F32)).astype(BF16)

        @pl.when(lax.rem(node, 2) == 0)
        def _():
            flat_ref[:, columns] = jnp.zeros((2 * head_dim, head_dim), BF16)

    def ring_copy(way, origin, c):
        return pltpu.make_async_remote_copy(
            src_ref=gather_ref.at[origin, c], dst_ref=gather_ref.at[origin, c],
            send_sem=ring_send.at[way], recv_sem=ring_recv.at[origin, c],
            device_id=(seq, neighbours[way]), device_id_type=MESH,
        )

    def passes(way, c):
        place = places[way]
        return jnp.logical_or(place + 1 < last, jnp.logical_and(place < last, c < keep))

    def send_own(way, begin, end):
        def one(c, carry):
            ring_copy(way, head, c).start()
            return carry

        lax.fori_loop(begin, end, one, 0)

    def relay(way, step, c):
        place = places[way]
        origin = origin_of(way, step)
        ring_copy(way, origin, c).wait_recv()

        @pl.when(passes(way, c))
        def _():
            ring_copy(way, origin, c).start()

        if helps:
            mine = fill + step * (tiles - keep) + c - keep

            @pl.when(jnp.logical_and(jnp.logical_and(place == last - 1, c >= keep), mine < keep))
            def _():
                ring_copy(way, head, mine).start()

            if step == last - 2:
                @pl.when(jnp.logical_and(place == last - 1, c == tiles - 1))
                def _():
                    send_own(way, min(fill + (last - 1) * (tiles - keep), keep), keep)

        @pl.when(jnp.logical_and(jnp.logical_and(place == step + 1, place < (last - 1 if helps else last)), c == tiles - 1))
        def _():
            send_own(way, first, tiles)

    def attn_tile(i):
        rows = pl.ds(pl.multiple_of(i * TILE, TILE), TILE)
        query = q_ref[rows, :]
        readout = dot(jnp.concatenate([query, query], axis=1), flat_ref[...], 1, 0)
        coeff = coeff_ref[rows, :]
        cross = jnp.zeros((TILE, head_dim), F32)
        for bit in range(seq_bits):
            level = local_bits + 1 + bit
            cross += coeff[:, level : level + 1] * readout[:, bit * head_dim : (bit + 1) * head_dim]
        total = total_ref[rows, :] + cross
        normed = total * lax.rsqrt(jnp.mean(total * total, axis=1, keepdims=True) + EPSILON)
        attn_ref[rows, :] = normed.astype(BF16)
        gather_ref[head, i] = normed.T.astype(BF16)

    lags = [jnp.minimum(LAG * place, pairs) for place in places]

    def sooner(way):
        return jnp.where(places[way] == last - 1, fill, first) if helps else first

    def middle(way):
        return jnp.logical_and(places[way] >= 1, places[way] < last)

    def produce(local):
        def step(t, carry):
            attn_tile(t)
            if local:
                local_tile(t + ahead)
            for way in range(2):
                @pl.when(jnp.logical_and(passes(way, t), jnp.logical_or(places[way] == 0, t < sooner(way))))
                def _():
                    ring_copy(way, head, t).start()
            for way in range(2):
                @pl.when(jnp.logical_and(middle(way), t >= lags[way]))
                def _():
                    relay(way, 0, t - lags[way])
            return carry
        return step

    with jax.named_scope("phase1a"):
        lax.fori_loop(0, tiles - ahead, produce(True), 0)
    with jax.named_scope("phase1b"):
        lax.fori_loop(tiles - ahead, tiles, produce(False), 0)
    if helps:
        start_helps(keep + 1, tiles)

    attn_copy = pltpu.make_async_copy(attn_ref, attn_hbm, out_sem.at[0])
    attn_copy.start()

    def joined(origin, q):
        return jnp.concatenate([gather_ref[origin, 4 * q + i] for i in range(4)], axis=1)

    def multiply(origin, q):
        rows = pl.ds(pl.multiple_of(q * (4 * TILE), 4 * TILE), 4 * TILE)
        acc_ref[origin] += dot(joined(origin, q), cot_ref[rows, :], 1, 0)

    def multiply_help(origin, q):
        rows = pl.ds(pl.multiple_of((q - keep // 4) * (4 * TILE), 4 * TILE), 4 * TILE)
        acc_ref[n_head + origin] += dot(joined(origin, q), help_ref[rows, :], 1, 0)

    def share_copy(slot, target):
        return pltpu.make_async_remote_copy(
            src_ref=share_ref.at[slot, pl.ds(target * rows_per, rows_per), :],
            dst_ref=shares_ref.at[slot, lax.rem(seq - target + n_seq, n_seq) - 1],
            send_sem=share_send.at[slot], recv_sem=share_recv.at[slot],
            device_id=(target, head), device_id_type=MESH,
        )

    def send_share(slot):
        share_ref[slot] = (acc_ref[slot] * scale).astype(BF16)
        for target in range(reducers):
            @pl.when(seq != target)
            def _():
                share_copy(slot, target).start()

    def final_copy(slot, block, origin, kind, owner):
        columns = pl.ds(owner * piece if piece < width else 0, piece)
        return pltpu.make_async_remote_copy(
            src_ref=final_ref.at[slot, :, columns] if piece < width else final_ref.at[slot],
            dst_ref=finals_ref.at[kind, pl.ds(pl.multiple_of(seq * rows_per, rows_per), rows_per), :],
            send_sem=final_send.at[slot], recv_sem=final_recv.at[kind],
            device_id=(block * owners + owner, origin), device_id_type=MESH,
        )

    def is_self(block, origin, owner):
        return jnp.logical_and(block * owners + owner == seq, origin == head)

    def reduce_share(slot, block, origin, kind):
        @pl.when(seq < reducers)
        def _():
            mine = pl.ds(pl.multiple_of(seq * rows_per, rows_per), rows_per)
            arrived = shares_ref.at[slot]
            pltpu.make_async_remote_copy(
                src_ref=arrived, dst_ref=arrived,
                send_sem=share_send.at[slot], recv_sem=share_recv.at[slot],
                device_id=(0, head), device_id_type=MESH,
            ).wait_recv()
            whole = acc_ref[slot, mine, :] * scale
            for source in range(n_seq - 1):
                whole += shares_ref[slot, source].astype(F32)
            final_ref[slot] = whole
            for owner in range(owners):
                @pl.when(jnp.logical_not(is_self(block, origin, owner)))
                def _():
                    final_copy(slot, block, origin, kind, owner).start()

                @pl.when(is_self(block, origin, owner))
                def _():
                    start = owner * piece if piece < width else 0
                    finals_ref[kind, mine, :] = final_ref[slot, :, pl.ds(start, piece)]

    loads[3].wait()

    def kept_quad(way, q):
        return jnp.logical_or(places[way] < last, 4 * q < keep)

    def arrive(way, step, q):
        for c in range(4):
            ring_copy(way, origin_of(way, step), 4 * q + c).wait_recv()

    def settle(u, carry):
        for way in range(2):
            c = tiles + u - lags[way]

            @pl.when(jnp.logical_and(middle(way), c < tiles))
            def _():
                relay(way, 0, c)
        q = u // 2

        @pl.when(lax.rem(u, 2) == 0)
        def _():
            multiply(head, q)

        @pl.when(lax.rem(u, 2) == 1)
        def _():
            for way in range(2):
                @pl.when(jnp.logical_and(places[way] > 0, kept_quad(way, q)))
                def _():
                    pl.when(places[way] == last)(lambda: arrive(way, 0, q))
                    multiply(origin_of(way, 0), q)
        return carry

    with jax.named_scope("settle"):
        lax.fori_loop(0, 2 * quads, settle, 0)

    def send_all(group):
        for condition, slot, _, _, _ in group:
            pl.when(condition)(functools.partial(send_share, slot))

    def reduce_all(group):
        for condition, *rest in group:
            pl.when(condition)(functools.partial(reduce_share, *rest))

    waiting = [(head >= 0, head, head, head, 0)]
    for way in range(2):
        waiting.append((places[way] > 0, origin_of(way, 0), head, origin_of(way, 0), 0))
    with jax.named_scope("share0"):
        send_all(waiting)
    if last > 1:
        nearest = []
        for way in range(2):
            origin = origin_of(way, last - 1)
            nearest.append((places[way] == last, origin, head, origin, 0))

            def near(q, carry):
                arrive(way, last - 1, q)
                multiply(origin, q)
                return carry

            @pl.when(places[way] == last)
            def _():
                with jax.named_scope("near"):
                    lax.fori_loop(0, keep // 4, near, 0)
                    send_share(origin)
        waiting += nearest
    every = list(waiting)

    for step in range(1, last - 1):
        helped = []
        if helps and step == 1:
            for way in range(2):
                for origin in (head, origin_of(way, 0)):
                    block = last if way == 0 else 0
                    helped.append((places[way] == last - 1, n_head + origin, block, origin, 1))

        def stream(q, carry):
            for i in range(4):
                c = 4 * q + i
                for way in range(2):
                    place = places[way]

                    @pl.when(jnp.logical_and(place > step, place < last))
                    def _():
                        relay(way, step, c)
            for way in range(2):
                place, origin = places[way], origin_of(way, step)

                @pl.when(jnp.logical_and(place > step, kept_quad(way, q)))
                def _():
                    pl.when(place == last)(lambda: arrive(way, step, q))
                    multiply(origin, q)

                if helps:
                    @pl.when(jnp.logical_and(place == last - 1, 4 * q >= keep))
                    def _():
                        multiply_help(origin, q)
            if helps and step == 1:
                for way in range(2):
                    @pl.when(jnp.logical_and(places[way] == last - 1, q == quads - 2))
                    def _():
                        for c in range(keep, tiles):
                            help_copy(way, c).wait_recv()
                        for group in range(keep // 4, quads):
                            multiply_help(head, group)
                            multiply_help(origin_of(way, 0), group)
                        send_share(n_head + head)
                        send_share(n_head + origin_of(way, 0))

            @pl.when(q == quads - 2)
            def _():
                reduce_all(waiting)
            return carry

        with jax.named_scope("stream%d" % step):
            lax.fori_loop(0, quads, stream, 0)

        done = []
        for way in range(2):
            place, origin = places[way], origin_of(way, step)
            done.append((place > step, origin, head, origin, 0))
            if helps:
                block = last if way == 0 else 0
                done.append((place == last - 1, n_head + origin, block, origin, 1))
        with jax.named_scope("share%d" % step):
            send_all(done)
        every += helped + done
        waiting = helped + done
    with jax.named_scope("reducelast"):
        reduce_all(waiting)

    with jax.named_scope("finals"):
        home = seq // owners
        at_end = jnp.logical_and(jnp.logical_or(home == 0, home == last), head != home)
        for kind in range(2 if helps else 1):
            plane = home if kind == 0 else jnp.where(home == 0, 1, last - 1)
            own = jnp.logical_and(seq < reducers, head == plane)
            expected = at_end if kind else seq >= 0
            for count, match in ((reducers - 1, own), (reducers, jnp.logical_not(own))):
                @pl.when(jnp.logical_and(expected, match))
                def _():
                    arrived = finals_ref.at[kind, pl.ds(0, count * rows_per), :]
                    pltpu.make_async_remote_copy(
                        src_ref=arrived, dst_ref=arrived,
                        send_sem=final_send.at[0], recv_sem=final_recv.at[kind],
                        device_id=(0, plane), device_id_type=MESH,
                    ).wait_recv()
        if helps:
            @pl.when(at_end)
            def _():
                finals_ref[0] += finals_ref[1]
        per = grad_ref.shape[1]
        if per == piece:
            grad_ref[...] = finals_ref[0]
        else:
            for owner in range(owners):
                @pl.when(lax.rem(seq, owners) == owner)
                def _():
                    grad_ref[...] = finals_ref[0][:, owner * per : (owner + 1) * per]

    with jax.named_scope("drain"):
        for block in range(n_seq - 1):
            @pl.when(seq == block)
            def _():
                sent = states_ref.at[pl.ds(0, n_seq - 1 - block)]
                pltpu.make_async_remote_copy(
                    src_ref=sent, dst_ref=sent,
                    send_sem=state_send.at[0], recv_sem=state_recv.at[0],
                    device_id=(0, head), device_id_type=MESH,
                ).wait_send()
        for way in range(2):
            if helps:
                @pl.when(places[way] == last)
                def _():
                    pltpu.make_async_remote_copy(
                        src_ref=help_ref, dst_ref=help_ref,
                        send_sem=help_send.at[0], recv_sem=help_recv.at[0],
                        device_id=(seq, left if way == 0 else right), device_id_type=MESH,
                    ).wait_send()
            for place in range(last):
                @pl.when(places[way] == place)
                def _():
                    count = tiles if place + 1 < last else keep
                    sent = gather_ref.at[pl.ds(0, place + 1), pl.ds(0, count)]
                    pltpu.make_async_remote_copy(
                        src_ref=sent, dst_ref=sent,
                        send_sem=ring_send.at[way], recv_sem=ring_recv.at[0, 0],
                        device_id=(seq, neighbours[way]), device_id_type=MESH,
                    ).wait_send()
        for condition, slot, block, origin, kind in every:
            @pl.when(condition)
            def _():
                def sent_shares(count):
                    sent = share_ref.at[slot, pl.ds(0, count * rows_per), :]
                    pltpu.make_async_remote_copy(
                        src_ref=sent, dst_ref=sent,
                        send_sem=share_send.at[slot], recv_sem=share_recv.at[slot],
                        device_id=(0, head), device_id_type=MESH,
                    ).wait_send()

                def sent_finals(count):
                    sent = finals_ref.at[0, pl.ds(0, count * rows_per), :]
                    pltpu.make_async_remote_copy(
                        src_ref=sent, dst_ref=sent,
                        send_sem=final_send.at[slot], recv_sem=final_recv.at[0],
                        device_id=(0, head), device_id_type=MESH,
                    ).wait_send()

                pl.when(seq < reducers)(lambda: sent_shares(reducers - 1))
                if reducers < n_seq:
                    pl.when(seq >= reducers)(lambda: sent_shares(reducers))
                near = jnp.logical_and(seq // owners == block, origin == head)
                pl.when(jnp.logical_and(seq < reducers, jnp.logical_not(near)))(lambda: sent_finals(owners))
                if owners > 1:
                    pl.when(jnp.logical_and(seq < reducers, near))(lambda: sent_finals(owners - 1))
        attn_copy.wait()


def finish(attn_ref, grad_ref, attn_out, grad_out, held_ref, sem):
    rows = attn_ref.shape[0] // 4
    parts = [pl.ds(i * rows, rows) for i in range(4)]
    takes = [pltpu.make_async_copy(attn_ref.at[part], held_ref.at[part], sem.at[0, i]) for i, part in enumerate(parts)]
    puts = [pltpu.make_async_copy(held_ref.at[part], attn_out.at[part], sem.at[1, i]) for i, part in enumerate(parts)]
    for take in takes:
        take.start()
    grad_out[...] = grad_ref[...].T
    for take, put in zip(takes, puts):
        take.wait()
        put.start()
    for put in puts:
        put.wait()


def body(n_seq, n_head, queries, keys, values, level_ids, level_table, out_cotangent):
    block_len, head_dim = queries.shape
    width = out_cotangent.shape[1]
    per = width * n_head // n_seq
    piece = per if per % 128 == 0 else width
    seq_bits = n_seq.bit_length() - 1
    tiles = block_len // TILE
    inner = tiles.bit_length() - 1
    rows_per = max(16, head_dim // n_seq)
    slots = 2 * n_head
    spare = max(1, tiles - kept_tiles(n_head, tiles))
    dma = pltpu.SemaphoreType.DMA
    vmem = pl.BlockSpec(memory_space=pltpu.VMEM)
    hbm = pl.BlockSpec(memory_space=pl.ANY)
    attn_out, grad = pl.pallas_call(
        functools.partial(kernel, n_seq, n_head),
        out_shape=(
            jax.ShapeDtypeStruct((block_len, head_dim), BF16),
            jax.ShapeDtypeStruct((head_dim, per), F32),
        ),
        in_specs=[hbm, hbm, hbm, vmem, vmem, hbm],
        out_specs=(hbm, vmem),
        scratch_shapes=[
            pltpu.VMEM((block_len, head_dim), BF16),
            pltpu.VMEM((block_len, head_dim), BF16),
            pltpu.VMEM((block_len, head_dim), BF16),
            pltpu.VMEM((block_len, width), BF16),
            pltpu.VMEM((TILE, TILE), jnp.int32),
            pltpu.VMEM((block_len, level_table.shape[1]), F32),
            pltpu.VMEM((block_len, head_dim), F32),
            pltpu.VMEM((tiles, head_dim, inner * head_dim), BF16),
            pltpu.VMEM((head_dim, head_dim), BF16),
            pltpu.VMEM((n_seq, head_dim, head_dim), BF16),
            pltpu.VMEM((2 * head_dim, seq_bits * head_dim), BF16),
            pltpu.VMEM((block_len, head_dim), BF16),
            pltpu.VMEM((n_head, tiles, head_dim, TILE), BF16),
            pltpu.VMEM((slots, head_dim, width), F32),
            pltpu.VMEM((slots, head_dim, width), BF16),
            pltpu.VMEM((slots, n_seq - 1, rows_per, width), BF16),
            pltpu.VMEM((slots, rows_per, width), F32),
            pltpu.VMEM((2, head_dim, piece), F32),
            pltpu.VMEM((spare * TILE, width), BF16),
            dma((4,)),
            dma((1,)),
            dma((1,)),
            dma((1,)),
            dma((2,)),
            dma((n_head, tiles)),
            dma((slots,)),
            dma((slots,)),
            dma((slots,)),
            dma((2,)),
            dma((1,)),
            dma((spare,)),
        ],
        compiler_params=pltpu.CompilerParams(
            collective_id=0, has_side_effects=True, vmem_limit_bytes=60 * 2**20
        ),
    )(queries, keys, values, level_ids[None, :], level_table.T, out_cotangent)
    return pl.pallas_call(
        finish,
        out_shape=(
            jax.ShapeDtypeStruct((block_len, head_dim), BF16),
            jax.ShapeDtypeStruct((per, head_dim), F32),
        ),
        in_specs=[hbm, vmem],
        out_specs=(hbm, vmem),
        scratch_shapes=[pltpu.VMEM((block_len, head_dim), BF16), dma((2, 4))],
    )(attn_out, grad)


def solution(mesh):
    in_specs = (
        P("seq", "head"),
        P("seq", "head"),
        P("seq", "head"),
        P("seq"),
        P(),
        P("seq", "head"),
    )
    out_specs = (P("seq", "head"), P("seq", "head"))
    return jax.shard_map(
        functools.partial(body, mesh.shape["seq"], mesh.shape["head"]),
        mesh=mesh, in_specs=in_specs, out_specs=out_specs, check_vma=False,
    )
```

time: 62.5 us -> 55.7 us (0.89)
  the two profiles are of different devices: /device:TPU:25 before, /device:TPU:17 now
where the time goes in v1:
time: 55.7 us; the launch traced here: 55.4 us
  Pallas kernels  54.8 us (98%)
  between operations  0.64 us (1%)
    pallas_call x1, Pallas kernels, body(): pl.pallas_call(functools.partial(kernel, n_seq, n_head), out_shape=(jax.S...  51.4 us
    pallas_call x1, Pallas kernels, body(): pl.pallas_call(finish, out_shape=(jax.ShapeDtypeStruct((block_len, head_d...  3.38 us

profile of v1, /device:TPU:17, one launch (start us, length us, event | category | flops | bytes accessed | tf_op | source)
XLA Modules:
  0.0 55.4 jit_solution(17479415714894639977)
XLA Ops:
  0.6 51.4 %shard_map.77 = (bf16[2048,128]{1,0:T(8,128)(2,1)}, f32[128,256]{1,0:T(8,128)}) custom-call(bf16[2048,128]{1,0:T(8,128)(2,1)} %q_hbm.1, bf16[2048,128]{1,0:T(8,128)(2,1)} %k_hbm.1, bf16[2048,128]{1,0:T(8,128)(2,1)} %v_hbm.1, s32[1,2048]{1,0:T(1,128)} %bitcast.2, f32[15,64]{1,0:T(8,128)} %bitcast.3, bf16[2048,512]{1,0:T(8,128)(2,1)} %cot_hbm.1), custom_call_target="tpu_custom_call" | custom-call | tf_op jit(solution)/shard_map/pallas_call | solution.py:619
  52.0 3.4 %shard_map.78 = (bf16[2048,128]{1,0:T(8,128)(2,1)}, f32[256,128]{1,0:T(8,128)}) custom-call(bf16[2048,128]{1,0:T(8,128)(2,1)} %get-tuple-element.4.attn_ref, f32[128,256]{1,0:T(8,128)} %get-tuple-element.5.grad_ref), custom_call_target="tpu_custom_call" | custom-call | tf_op jit(solution)/shard_map/pallas_call | solution.py:664

commit v2 on v1

v2 whole, which is shorter than its diff:
```python
import functools

import jax
import jax.numpy as jnp
from jax import lax
from jax.experimental import pallas as pl
from jax.experimental.pallas import tpu as pltpu
from jax.sharding import PartitionSpec as P

EPSILON = 1e-06
TILE = 128
KEEP = 12
EARLY = 2
AHEAD = 10
LAG = 4
BURST = 2
MESH = pl.DeviceIdType.MESH
F32 = jnp.float32
BF16 = jnp.bfloat16


def dot(a, b, ca, cb):
    return lax.dot_general(a, b, (((ca,), (cb,)), ((), ())), preferred_element_type=F32)


def tile_levels(tile):
    row = lax.broadcasted_iota(jnp.int32, (tile, tile), 0)
    col = lax.broadcasted_iota(jnp.int32, (tile, tile), 1)
    apart = jnp.bitwise_xor(row, col)
    levels = jnp.zeros((tile, tile), jnp.int32)
    for bit in range(tile.bit_length() - 1):
        levels = levels + (jnp.right_shift(apart, bit) > 0).astype(jnp.int32)
    return jnp.where(col <= row, levels, -1)


def kept_tiles(n_head, tiles):
    return tiles * KEEP // 16 if n_head >= 4 else tiles


def kernel(
    n_seq, n_head,
    q_hbm, k_hbm, v_hbm, ids_hbm, table_hbm, cot_hbm,
    attn_ref, grad_ref,
    q_ref, k_ref, v_ref, cot_ref, ids_ref, table_ref, levels_ref, coeff_ref, total_ref, sib_ref,
    state_ref, states_ref, flat_ref, gather_ref, acc_ref,
    share_ref, shares_ref, final_ref, finals_ref, help_ref,
    load_sem, state_send, state_recv, ring_send, ring_recv,
    share_send, share_recv, final_send, final_recv, help_send, help_recv,
):
    seq, head = lax.axis_index("seq"), lax.axis_index("head")
    block_len, head_dim = q_ref.shape
    width = cot_ref.shape[1]
    tiles = block_len // TILE
    pairs = tiles // 2
    tile_bits = TILE.bit_length() - 1
    local_bits = block_len.bit_length() - 1
    inner = local_bits - tile_bits
    seq_bits = n_seq.bit_length() - 1
    owners = n_seq // n_head
    rows_per = max(16, head_dim // n_seq)
    reducers = head_dim // rows_per
    piece = finals_ref.shape[2]
    last = n_head - 1
    keep = kept_tiles(n_head, tiles)
    helps = keep < tiles
    quads = tiles // 4
    early = min(EARLY, tiles)
    ahead = min(AHEAD, tiles)
    scale = (block_len * n_seq) ** (-0.5)

    loads = [
        pltpu.make_async_copy(src, dst, load_sem.at[i])
        for i, (src, dst) in enumerate(
            [
                (k_hbm, k_ref), (v_hbm, v_ref), (table_hbm, table_ref), (ids_hbm, ids_ref),
                (q_hbm, q_ref), (cot_hbm, cot_ref),
            ]
        )
    ]
    for load in loads:
        load.start()

    barrier = pltpu.get_barrier_semaphore()

    def greet(device):
        pl.semaphore_signal(barrier, inc=1, device_id=device, device_id_type=MESH)

    for step in range(1, n_seq):
        greet((lax.rem(seq + step, n_seq), head))
    pl.when(head > 0)(lambda: greet((seq, head - 1)))
    pl.when(head < n_head - 1)(lambda: greet((seq, head + 1)))

    levels_ref[...] = tile_levels(TILE)
    for load in loads[:4]:
        load.wait()
    table = table_ref[...]
    high = table.astype(BF16)
    rest = table - high.astype(F32)
    mid = rest.astype(BF16)
    low = (rest - mid.astype(F32)).astype(BF16)
    table3 = jnp.concatenate([high, mid, low], axis=1)

    nodes = [
        dot(k_ref[pl.ds(i * TILE, TILE), :], v_ref[pl.ds(i * TILE, TILE), :], 0, 0)
        for i in range(tiles)
    ]
    for bit in range(inner):
        for i in range(tiles):
            place = (i >> bit) ^ 1
            value = nodes[place].astype(BF16) if (i >> bit) & 1 else jnp.zeros((head_dim, head_dim), BF16)
            sib_ref[i, :, pl.ds(bit * head_dim, head_dim)] = value
        nodes = [nodes[2 * i] + nodes[2 * i + 1] for i in range(len(nodes) // 2)]
    state_ref[...] = nodes[0].astype(BF16)

    loads[4].wait()

    def local_tile(i):
        rows = pl.ds(pl.multiple_of(i * TILE, TILE), TILE)
        row_ids = lax.broadcasted_iota(jnp.int32, (table.shape[1], TILE), 0)
        onehot = (row_ids == ids_ref[:, rows]).astype(F32).astype(BF16)
        coeff = dot(jnp.concatenate([onehot] * 3, axis=0), table3, 0, 1)
        coeff_ref[rows, :] = coeff
        levels = levels_ref[...]
        weights = jnp.zeros((TILE, TILE), F32)
        for level in range(tile_bits + 1):
            weights = jnp.where(levels == level, coeff[:, level : level + 1], weights)
        query = q_ref[rows, :]
        scores = dot(query, k_ref[rows, :], 1, 1)
        total = dot((weights * scores).astype(BF16), v_ref[rows, :], 1, 0)
        readout = dot(query, sib_ref[i], 1, 0)
        for bit in range(inner):
            level = tile_bits + 1 + bit
            total += coeff[:, level : level + 1] * readout[:, bit * head_dim : (bit + 1) * head_dim]
        total_ref[rows, :] = total

    def local_tiles(start, stop):
        def one(i, carry):
            local_tile(jnp.where(head < n_head // 2, i, tiles - 1 - i))
            return carry

        lax.fori_loop(start, stop, one, 0, unroll=True)

    with jax.named_scope("local0"):
        local_tiles(0, early)

    with jax.named_scope("barrier"):
        pl.semaphore_wait(barrier, n_seq - 1 + jnp.minimum(head, 1) + jnp.minimum(last - head, 1))

    def state_copy(target):
        return pltpu.make_async_remote_copy(
            src_ref=state_ref, dst_ref=states_ref.at[seq],
            send_sem=state_send.at[0], recv_sem=state_recv.at[0],
            device_id=(target, head), device_id_type=MESH,
        )

    for target in range(1, n_seq):
        @pl.when(seq < target)
        def _():
            state_copy(target).start()

    right, left = lax.rem(head + 1, n_head), lax.rem(head + n_head - 1, n_head)
    neighbours = (right, left)
    places = (head, last - head)

    half = n_head // 2
    spare = tiles - keep

    def origin_of(way, distance):
        return head - distance if way == 0 else head + distance

    def tile_of(origin, i):
        return jnp.where(origin < half, i, tiles - 1 - i)

    def quad_of(origin, j):
        return jnp.where(origin < half, j, quads - 1 - j)

    def kept(way, c):
        return c >= spare if way == 0 else c < keep

    def kept_quad(way, q):
        return 4 * q >= spare if way == 0 else 4 * q < keep

    def help_copy(way, i):
        return pltpu.make_async_remote_copy(
            src_ref=cot_hbm.at[pl.ds(i * TILE if way == 0 else (keep + i) * TILE, TILE), :],
            dst_ref=help_ref.at[pl.ds(i * TILE, TILE), :],
            send_sem=help_send.at[0], recv_sem=help_recv.at[i],
            device_id=(seq, left if way == 0 else right), device_id_type=MESH,
        )

    for way in range(2):
        @pl.when(places[way] == last)
        def _():
            for i in range(spare):
                help_copy(way, i).start()

    with jax.named_scope("local1"):
        local_tiles(early, ahead)
    acc_ref[...] = jnp.zeros_like(acc_ref)

    with jax.named_scope("states"):
        for block in range(1, n_seq):
            @pl.when(seq == block)
            def _():
                arrived = states_ref.at[pl.ds(0, block)]
                pltpu.make_async_remote_copy(
                    src_ref=arrived, dst_ref=arrived,
                    send_sem=state_send.at[0], recv_sem=state_recv.at[0],
                    device_id=(0, head), device_id_type=MESH,
                ).wait_recv()

    for bit in range(seq_bits):
        span = 2**bit
        node = seq // span
        columns = pl.ds(bit * head_dim, head_dim)

        @pl.when(lax.rem(node, 2) == 1)
        def _():
            total = jnp.zeros((head_dim, head_dim), F32)
            for offset in range(span):
                total += states_ref[(node - 1) * span + offset].astype(F32)
            upper = total.astype(BF16)
            flat_ref[pl.ds(0, head_dim), columns] = upper
            flat_ref[pl.ds(head_dim, head_dim), columns] = (total - upper.astype(F32)).astype(BF16)

        @pl.when(lax.rem(node, 2) == 0)
        def _():
            flat_ref[:, columns] = jnp.zeros((2 * head_dim, head_dim), BF16)

    def ring_copy(way, origin, c):
        return pltpu.make_async_remote_copy(
            src_ref=gather_ref.at[origin, c], dst_ref=gather_ref.at[origin, c],
            send_sem=ring_send.at[way], recv_sem=ring_recv.at[origin, c],
            device_id=(seq, neighbours[way]), device_id_type=MESH,
        )

    def passes(way, c):
        place = places[way]
        return jnp.logical_or(place + 1 < last, jnp.logical_and(place < last, kept(way, c)))

    def relay(way, distance, i):
        origin = origin_of(way, distance)
        c = tile_of(origin, i)
        ring_copy(way, origin, c).wait_recv()

        @pl.when(passes(way, c))
        def _():
            ring_copy(way, origin, c).start()

    def attn_tile(i):
        rows = pl.ds(pl.multiple_of(i * TILE, TILE), TILE)
        query = q_ref[rows, :]
        readout = dot(jnp.concatenate([query, query], axis=1), flat_ref[...], 1, 0)
        coeff = coeff_ref[rows, :]
        cross = jnp.zeros((TILE, head_dim), F32)
        for bit in range(seq_bits):
            level = local_bits + 1 + bit
            cross += coeff[:, level : level + 1] * readout[:, bit * head_dim : (bit + 1) * head_dim]
        total = total_ref[rows, :] + cross
        normed = total * lax.rsqrt(jnp.mean(total * total, axis=1, keepdims=True) + EPSILON)
        attn_ref[rows, :] = normed.astype(BF16)
        gather_ref[head, i] = normed.T.astype(BF16)

    def middle(way):
        return jnp.logical_and(places[way] >= 2, places[way] < last)

    early_tiles = BURST * spare

    def produce(local):
        def step(t, carry):
            tile = tile_of(head, t)
            attn_tile(tile)
            if local:
                local_tile(tile_of(head, t + ahead))
            for way in range(2):
                @pl.when(passes(way, tile))
                def _():
                    ring_copy(way, head, tile).start()
            if not local:
                for way in range(2):
                    @pl.when(jnp.logical_and(middle(way), t >= keep))
                    def _():
                        for i in range(BURST):
                            relay(way, 1, BURST * (t - keep) + i)
            return carry
        return step

    with jax.named_scope("phase1a"):
        lax.fori_loop(0, tiles - ahead, produce(True), 0)
    with jax.named_scope("phase1b"):
        lax.fori_loop(tiles - ahead, tiles, produce(False), 0)

    def joined(origin, q):
        return jnp.concatenate([gather_ref[origin, 4 * q + i] for i in range(4)], axis=1)

    def multiply(origin, q):
        rows = pl.ds(pl.multiple_of(q * (4 * TILE), 4 * TILE), 4 * TILE)
        acc_ref[origin] += dot(joined(origin, q), cot_ref[rows, :], 1, 0)

    def multiply_help(way, origin, i):
        rows = pl.ds(pl.multiple_of(i * (4 * TILE), 4 * TILE), 4 * TILE)
        acc_ref[n_head + origin] += dot(joined(origin, i if way == 0 else keep // 4 + i), help_ref[rows, :], 1, 0)

    def share_copy(slot, target):
        return pltpu.make_async_remote_copy(
            src_ref=share_ref.at[slot, pl.ds(target * rows_per, rows_per), :],
            dst_ref=shares_ref.at[slot, lax.rem(seq - target + n_seq, n_seq) - 1],
            send_sem=share_send.at[slot], recv_sem=share_recv.at[slot],
            device_id=(target, head), device_id_type=MESH,
        )

    def send_share(slot):
        share_ref[slot] = (acc_ref[slot] * scale).astype(BF16)
        for target in range(reducers):
            @pl.when(seq != target)
            def _():
                share_copy(slot, target).start()

    def final_copy(slot, block, origin, kind, owner):
        columns = pl.ds(owner * piece if piece < width else 0, piece)
        return pltpu.make_async_remote_copy(
            src_ref=final_ref.at[slot, :, columns] if piece < width else final_ref.at[slot],
            dst_ref=finals_ref.at[kind, pl.ds(pl.multiple_of(seq * rows_per, rows_per), rows_per), :],
            send_sem=final_send.at[slot], recv_sem=final_recv.at[kind],
            device_id=(block * owners + owner, origin), device_id_type=MESH,
        )

    def is_self(block, origin, owner):
        return jnp.logical_and(block * owners + owner == seq, origin == head)

    def reduce_share(slot, block, origin, kind):
        @pl.when(seq < reducers)
        def _():
            mine = pl.ds(pl.multiple_of(seq * rows_per, rows_per), rows_per)
            arrived = shares_ref.at[slot]
            pltpu.make_async_remote_copy(
                src_ref=arrived, dst_ref=arrived,
                send_sem=share_send.at[slot], recv_sem=share_recv.at[slot],
                device_id=(0, head), device_id_type=MESH,
            ).wait_recv()
            whole = acc_ref[slot, mine, :] * scale
            for source in range(n_seq - 1):
                whole += shares_ref[slot, source].astype(F32)
            final_ref[slot] = whole
            for owner in range(owners):
                @pl.when(jnp.logical_not(is_self(block, origin, owner)))
                def _():
                    final_copy(slot, block, origin, kind, owner).start()

                @pl.when(is_self(block, origin, owner))
                def _():
                    start = owner * piece if piece < width else 0
                    finals_ref[kind, mine, :] = final_ref[slot, :, pl.ds(start, piece)]

    loads[5].wait()

    def arrive(way, origin, q):
        for c in range(4):
            ring_copy(way, origin, 4 * q + c).wait_recv()

    def helper(way):
        return jnp.logical_and(places[way] == last - 1, helps)

    def block_of(way):
        return last if way == 0 else 0

    def every_group(distance, act):
        @pl.when(distance == 0)
        def _():
            act(head, head, head, 0)
            if helps:
                for way in range(2):
                    pl.when(helper(way))(functools.partial(act, n_head + head, block_of(way), head, 1))

        for way in range(2):
            origin = origin_of(way, distance)

            @pl.when(jnp.logical_and(distance > 0, distance < places[way]))
            def _():
                act(origin, head, origin, 0)
                if helps:
                    pl.when(helper(way))(functools.partial(act, n_head + origin, block_of(way), origin, 1))

    began = early_tiles
    if last > 3:
        began = tiles
        for way in range(2):
            def rest(i, carry):
                relay(way, 1, i)
                return carry

            def more(n, carry):
                relay(way, 2 + n // tiles, lax.rem(n, tiles))
                return carry

            @pl.when(middle(way))
            def _():
                lax.fori_loop(early_tiles, tiles, rest, 0)
                lax.fori_loop(0, (places[way] - 2) * tiles, more, 0)

    farthest = jnp.maximum(places[0], places[1])

    def flow(u, carry):
        for way in range(2):
            place, origin = places[way], block_of(1 - way)
            i = u - 1 - LAG * (place - 1)

            if began < tiles:
                @pl.when(jnp.logical_and(middle(way), u < tiles - began))
                def _():
                    relay(way, 1, began + u)

            @pl.when(jnp.logical_and(jnp.logical_and(place > 0, place < last), jnp.logical_and(i >= 0, i < tiles)))
            def _():
                relay(way, place, i)

        for way in range(2):
            place, origin = places[way], block_of(1 - way)
            i = u - 1 - LAG * (place - 1)
            j = i // 4
            q = quad_of(origin, j)

            @pl.when(jnp.logical_and(jnp.logical_and(place > 0, i - 4 * j == 3), jnp.logical_and(i >= 0, i < tiles)))
            def _():
                @pl.when(jnp.logical_or(place < last, kept_quad(way, q)))
                def _():
                    pl.when(place == last)(functools.partial(arrive, way, origin, q))
                    multiply(origin, q)
                if helps:
                    @pl.when(jnp.logical_and(helper(way), jnp.logical_not(kept_quad(way, q))))
                    def _():
                        multiply_help(way, origin, 0)
                        send_share(n_head + origin)
                pl.when(j == quads - 1)(functools.partial(send_share, origin))

        distance = u // quads
        j = u - quads * distance

        @pl.when(distance == 0)
        def _():
            multiply(head, quad_of(head, j))

        for way in range(2):
            place, origin = places[way], origin_of(way, distance)
            q = quad_of(origin, j)

            @pl.when(jnp.logical_and(jnp.logical_and(distance > 0, distance < place), jnp.logical_or(place < last, kept_quad(way, q))))
            def _():
                pl.when(place == last)(functools.partial(arrive, way, origin, q))
                multiply(origin, q)

            if helps:
                @pl.when(jnp.logical_and(helper(way), jnp.logical_and(distance < place, j == quads - 1)))
                def _():
                    @pl.when(distance == 0)
                    def _():
                        for i in range(spare):
                            help_copy(way, i).wait_recv()
                    multiply_help(way, origin, 0)

        @pl.when(j == quads - 1)
        def _():
            every_group(distance, lambda slot, *_: send_share(slot))
            pl.when(jnp.logical_and(farthest == last, distance >= 2))(lambda: every_group(distance - 2, reduce_share))
        return carry

    with jax.named_scope("flow"):
        lax.fori_loop(0, jnp.maximum(tiles + 1 + LAG * (farthest - 1), quads * (farthest + 2)), flow, 0)

    ends = []
    for way in range(2):
        place, origin = places[way], block_of(1 - way)
        if helps:
            ends.append((helper(way), n_head + origin, block_of(way), origin, 1))
    for way in range(2):
        place, origin = places[way], block_of(1 - way)
        ends.append((place > 0, origin, head, origin, 0))
    with jax.named_scope("reducelast"):
        @pl.when(farthest < last)
        def _():
            def one(distance, carry):
                every_group(distance, reduce_share)
                return carry

            lax.fori_loop(0, farthest, one, 0)

        for condition, *rest in ends[:-2]:
            pl.when(condition)(functools.partial(reduce_share, *rest))
        closer = places[0] <= places[1]
        for flip, pair in ((closer, ends[-2:]), (jnp.logical_not(closer), ends[-2:][::-1])):
            @pl.when(flip)
            def _():
                for condition, *rest in pair:
                    pl.when(condition)(functools.partial(reduce_share, *rest))

    with jax.named_scope("finals"):
        home = seq // owners
        at_end = jnp.logical_and(jnp.logical_or(home == 0, home == last), head != home)
        for kind in range(2 if helps else 1):
            plane = home if kind == 0 else jnp.where(home == 0, 1, last - 1)
            own = jnp.logical_and(seq < reducers, head == plane)
            expected = at_end if kind else seq >= 0
            for count, match in ((reducers - 1, own), (reducers, jnp.logical_not(own))):
                @pl.when(jnp.logical_and(expected, match))
                def _():
                    arrived = finals_ref.at[kind, pl.ds(0, count * rows_per), :]
                    pltpu.make_async_remote_copy(
                        src_ref=arrived, dst_ref=arrived,
                        send_sem=final_send.at[0], recv_sem=final_recv.at[kind],
                        device_id=(0, plane), device_id_type=MESH,
                    ).wait_recv()
        if helps:
            @pl.when(at_end)
            def _():
                finals_ref[0] += finals_ref[1]
        per = grad_ref.shape[1]
        if per == piece:
            grad_ref[...] = finals_ref[0]
        else:
            for owner in range(owners):
                @pl.when(lax.rem(seq, owners) == owner)
                def _():
                    grad_ref[...] = finals_ref[0][:, owner * per : (owner + 1) * per]

    with jax.named_scope("drain"):
        for block in range(n_seq - 1):
            @pl.when(seq == block)
            def _():
                sent = states_ref.at[pl.ds(0, n_seq - 1 - block)]
                pltpu.make_async_remote_copy(
                    src_ref=sent, dst_ref=sent,
                    send_sem=state_send.at[0], recv_sem=state_recv.at[0],
                    device_id=(0, head), device_id_type=MESH,
                ).wait_send()
        for way in range(2):
            if helps:
                @pl.when(places[way] == last)
                def _():
                    pltpu.make_async_remote_copy(
                        src_ref=help_ref, dst_ref=help_ref,
                        send_sem=help_send.at[0], recv_sem=help_recv.at[0],
                        device_id=(seq, left if way == 0 else right), device_id_type=MESH,
                    ).wait_send()
            for place in range(last):
                @pl.when(places[way] == place)
                def _():
                    count = tiles if place + 1 < last else keep
                    sent = gather_ref.at[pl.ds(0, place + 1), pl.ds(0, count)]
                    pltpu.make_async_remote_copy(
                        src_ref=sent, dst_ref=sent,
                        send_sem=ring_send.at[way], recv_sem=ring_recv.at[0, 0],
                        device_id=(seq, neighbours[way]), device_id_type=MESH,
                    ).wait_send()
        def drain(slot, block, origin, kind):
            def sent_shares(count):
                sent = share_ref.at[slot, pl.ds(0, count * rows_per), :]
                pltpu.make_async_remote_copy(
                    src_ref=sent, dst_ref=sent,
                    send_sem=share_send.at[slot], recv_sem=share_recv.at[slot],
                    device_id=(0, head), device_id_type=MESH,
                ).wait_send()

            def sent_finals(count):
                sent = finals_ref.at[0, pl.ds(0, count * rows_per), :]
                pltpu.make_async_remote_copy(
                    src_ref=sent, dst_ref=sent,
                    send_sem=final_send.at[slot], recv_sem=final_recv.at[0],
                    device_id=(0, head), device_id_type=MESH,
                ).wait_send()

            pl.when(seq < reducers)(lambda: sent_shares(reducers - 1))
            if reducers < n_seq:
                pl.when(seq >= reducers)(lambda: sent_shares(reducers))
            near = jnp.logical_and(seq // owners == block, origin == head)
            pl.when(jnp.logical_and(seq < reducers, jnp.logical_not(near)))(lambda: sent_finals(owners))
            if owners > 1:
                pl.when(jnp.logical_and(seq < reducers, near))(lambda: sent_finals(owners - 1))

        for origin in range(n_head):
            drain(origin, head, origin, 0)
        if helps:
            for way in range(2):
                for origin in range(n_head):
                    @pl.when(jnp.logical_and(helper(way), origin != block_of(way)))
                    def _():
                        drain(n_head + origin, block_of(way), origin, 1)


def finish(attn_ref, grad_ref, attn_out, grad_out, turned_ref, sem):
    attn_copy = pltpu.make_async_copy(attn_ref, attn_out, sem.at[0])
    attn_copy.start()
    turned_ref[...] = grad_ref[...].T
    grad_copy = pltpu.make_async_copy(turned_ref, grad_out, sem.at[1])
    grad_copy.start()
    attn_copy.wait()
    grad_copy.wait()


def body(n_seq, n_head, queries, keys, values, level_ids, level_table, out_cotangent):
    block_len, head_dim = queries.shape
    width = out_cotangent.shape[1]
    per = width * n_head // n_seq
    piece = per if per % 128 == 0 else width
    seq_bits = n_seq.bit_length() - 1
    tiles = block_len // TILE
    inner = tiles.bit_length() - 1
    rows_per = max(16, head_dim // n_seq)
    slots = 2 * n_head
    spare = max(4, tiles - kept_tiles(n_head, tiles))
    dma = pltpu.SemaphoreType.DMA
    vmem = pl.BlockSpec(memory_space=pltpu.VMEM)
    hbm = pl.BlockSpec(memory_space=pltpu.HBM)
    attn_out, grad = pl.pallas_call(
        functools.partial(kernel, n_seq, n_head),
        out_shape=(
            pltpu.VMEM((block_len, head_dim), BF16),
            pltpu.VMEM((head_dim, per), F32),
        ),
        in_specs=[hbm] * 6,
        out_specs=(vmem, vmem),
        scratch_shapes=[
            pltpu.VMEM((block_len, head_dim), BF16),
            pltpu.VMEM((block_len, head_dim), BF16),
            pltpu.VMEM((block_len, head_dim), BF16),
            pltpu.VMEM((block_len, width), BF16),
            pltpu.VMEM((1, block_len), jnp.int32),
            pltpu.VMEM(level_table.shape[::-1], F32),
            pltpu.VMEM((TILE, TILE), jnp.int32),
            pltpu.VMEM((block_len, level_table.shape[1]), F32),
            pltpu.VMEM((block_len, head_dim), F32),
            pltpu.VMEM((tiles, head_dim, inner * head_dim), BF16),
            pltpu.VMEM((head_dim, head_dim), BF16),
            pltpu.VMEM((n_seq, head_dim, head_dim), BF16),
            pltpu.VMEM((2 * head_dim, seq_bits * head_dim), BF16),
            pltpu.VMEM((n_head, tiles, head_dim, TILE), BF16),
            pltpu.VMEM((slots, head_dim, width), F32),
            pltpu.VMEM((slots, head_dim, width), BF16),
            pltpu.VMEM((slots, n_seq - 1, rows_per, width), BF16),
            pltpu.VMEM((slots, rows_per, width), F32),
            pltpu.VMEM((2, head_dim, piece), F32),
            pltpu.VMEM((spare * TILE, width), BF16),
            dma((6,)),
            dma((1,)),
            dma((1,)),
            dma((2,)),
            dma((n_head, tiles)),
            dma((slots,)),
            dma((slots,)),
            dma((slots,)),
            dma((2,)),
            dma((1,)),
            dma((spare,)),
        ],
        compiler_params=pltpu.CompilerParams(
            collective_id=0, has_side_effects=True, vmem_limit_bytes=60 * 2**20
        ),
    )(queries, keys, values, level_ids[None, :], level_table.T, out_cotangent)
    return pl.pallas_call(
        finish,
        out_shape=(
            jax.ShapeDtypeStruct((block_len, head_dim), BF16),
            jax.ShapeDtypeStruct((per, head_dim), F32),
        ),
        in_specs=[vmem, vmem],
        out_specs=(hbm, hbm),
        scratch_shapes=[pltpu.VMEM((per, head_dim), F32), dma((2,))],
        compiler_params=pltpu.CompilerParams(vmem_limit_bytes=4 * 2**20),
    )(attn_out, grad)


def solution(mesh):
    in_specs = (
        P("seq", "head"),
        P("seq", "head"),
        P("seq", "head"),
        P("seq"),
        P(),
        P("seq", "head"),
    )
    out_specs = (P("seq", "head"), P("seq", "head"))
    return jax.shard_map(
        functools.partial(body, mesh.shape["seq"], mesh.shape["head"]),
        mesh=mesh, in_specs=in_specs, out_specs=out_specs, check_vma=False,
    )
```

time: 55.7 us -> 48 us (0.86)
  the two profiles are of different devices: /device:TPU:17 before, /device:TPU:7 now
where the time goes in v2:
time: 48 us; the launch traced here: 47.8 us
  Pallas kernels  47.2 us (98%)
  between operations  0.64 us (1%)
    pallas_call x1, Pallas kernels, body(): pl.pallas_call(functools.partial(kernel, n_seq, n_head), out_shape=(pltpu...  46.3 us

profile of v2, /device:TPU:7, one launch (start us, length us, event | category | flops | bytes accessed | tf_op | source)
XLA Modules:
  0.0 47.8 jit_solution(15875734604857079893)
XLA Ops:
  0.6 46.3 %shard_map.77 = (bf16[2048,128]{1,0:T(8,128)(2,1)S(1)}, f32[128,256]{1,0:T(8,128)S(1)}) custom-call(bf16[2048,128]{1,0:T(8,128)(2,1)} %q_hbm.1, bf16[2048,128]{1,0:T(8,128)(2,1)} %k_hbm.1, bf16[2048,128]{1,0:T(8,128)(2,1)} %v_hbm.1, s32[1,2048]{1,0:T(1,128)} %bitcast.2, f32[15,64]{1,0:T(8,128)} %bitcast.3, bf16[2048,512]{1,0:T(8,128)(2,1)} %cot_hbm.1), custom_call_target="tpu_custom_call" | custom-call | tf_op jit(solution)/shard_map/pallas_call | solution.py:613
  47.0 0.8 %shard_map.78 = (bf16[2048,128]{1,0:T(8,128)(2,1)}, f32[256,128]{1,0:T(8,128)}) custom-call(bf16[2048,128]{1,0:T(8,128)(2,1)S(1)} %get-tuple-element.4.attn_ref, f32[128,256]{1,0:T(8,128)S(1)} %get-tuple-element.5.grad_ref), custom_call_target="tpu_custom_call" | custom-call | tf_op jit(solution)/shard_map/pallas_call | solution.py:658

commit v3 on v2

--- a/solution.py
+++ b/solution.py
@@ -10,9 +10,9 @@
 EPSILON = 1e-06
 TILE = 128
 KEEP = 12
-EARLY = 2
-AHEAD = 10
-LAG = 4
+AHEAD = 8
+LEAD = 4
+LAG = 6
 BURST = 2
 MESH = pl.DeviceIdType.MESH
 F32 = jnp.float32
@@ -64,8 +64,8 @@
     keep = kept_tiles(n_head, tiles)
     helps = keep < tiles
     quads = tiles // 4
-    early = min(EARLY, tiles)
     ahead = min(AHEAD, tiles)
+    lead = min(LEAD, ahead)
     scale = (block_len * n_seq) ** (-0.5)
 
     loads = [
@@ -77,7 +77,7 @@
             ]
         )
     ]
-    for load in loads:
+    for load in loads[:4]:
         load.start()
 
     barrier = pltpu.get_barrier_semaphore()
@@ -91,8 +91,11 @@
     pl.when(head < n_head - 1)(lambda: greet((seq, head + 1)))
 
     levels_ref[...] = tile_levels(TILE)
-    for load in loads[:4]:
-        load.wait()
+    with jax.named_scope("kv"):
+        for load in loads[:4]:
+            load.wait()
+    for load in loads[4:]:
+        load.start()
     table = table_ref[...]
     high = table.astype(BF16)
     rest = table - high.astype(F32)
@@ -112,7 +115,6 @@
         nodes = [nodes[2 * i] + nodes[2 * i + 1] for i in range(len(nodes) // 2)]
     state_ref[...] = nodes[0].astype(BF16)
 
-    loads[4].wait()
 
     def local_tile(i):
         rows = pl.ds(pl.multiple_of(i * TILE, TILE), TILE)
@@ -135,13 +137,10 @@
 
     def local_tiles(start, stop):
         def one(i, carry):
-            local_tile(jnp.where(head < n_head // 2, i, tiles - 1 - i))
+            local_tile(tile_of(head, i))
             return carry
 
         lax.fori_loop(start, stop, one, 0, unroll=True)
-
-    with jax.named_scope("local0"):
-        local_tiles(0, early)
 
     with jax.named_scope("barrier"):
         pl.semaphore_wait(barrier, n_seq - 1 + jnp.minimum(head, 1) + jnp.minimum(last - head, 1))
@@ -153,10 +152,17 @@
             device_id=(target, head), device_id_type=MESH,
         )
 
-    for target in range(1, n_seq):
-        @pl.when(seq < target)
-        def _():
-            state_copy(target).start()
+    def partner(k):
+        place = 0
+        for bit in range(seq_bits):
+            mine = lax.rem(seq // 2**bit, 2)
+            place += 2**bit * (1 - mine if (k >> bit) & 1 else mine)
+        return place
+
+    for k in range(n_seq - 1, 0, -1):
+        @pl.when(seq < partner(k))
+        def _():
+            state_copy(partner(k)).start()
 
     right, left = lax.rem(head + 1, n_head), lax.rem(head + n_head - 1, n_head)
     neighbours = (right, left)
@@ -168,11 +174,15 @@
     def origin_of(way, distance):
         return head - distance if way == 0 else head + distance
 
+    def upward(origin):
+        inside = jnp.logical_and(origin > 0, origin < half)
+        return jnp.logical_or(inside, origin == last)
+
     def tile_of(origin, i):
-        return jnp.where(origin < half, i, tiles - 1 - i)
+        return jnp.where(upward(origin), i, tiles - 1 - i)
 
     def quad_of(origin, j):
-        return jnp.where(origin < half, j, quads - 1 - j)
+        return jnp.where(upward(origin), j, quads - 1 - j)
 
     def kept(way, c):
         return c >= spare if way == 0 else c < keep
@@ -184,7 +194,7 @@
         return pltpu.make_async_remote_copy(
             src_ref=cot_hbm.at[pl.ds(i * TILE if way == 0 else (keep + i) * TILE, TILE), :],
             dst_ref=help_ref.at[pl.ds(i * TILE, TILE), :],
-            send_sem=help_send.at[0], recv_sem=help_recv.at[i],
+            send_sem=help_send.at[0], recv_sem=help_recv.at[0],
             device_id=(seq, left if way == 0 else right), device_id_type=MESH,
         )
 
@@ -194,8 +204,9 @@
             for i in range(spare):
                 help_copy(way, i).start()
 
+    loads[4].wait()
     with jax.named_scope("local1"):
-        local_tiles(early, ahead)
+        local_tiles(0, ahead)
     acc_ref[...] = jnp.zeros_like(acc_ref)
 
     with jax.named_scope("states"):
@@ -230,7 +241,7 @@
     def ring_copy(way, origin, c):
         return pltpu.make_async_remote_copy(
             src_ref=gather_ref.at[origin, c], dst_ref=gather_ref.at[origin, c],
-            send_sem=ring_send.at[way], recv_sem=ring_recv.at[origin, c],
+            send_sem=ring_send.at[way], recv_sem=ring_recv.at[origin - way, c],
             device_id=(seq, neighbours[way]), device_id_type=MESH,
         )
 
@@ -266,17 +277,17 @@
 
     early_tiles = BURST * spare
 
-    def produce(local):
+    def produce(local, relaying):
         def step(t, carry):
             tile = tile_of(head, t)
             attn_tile(tile)
             if local:
-                local_tile(tile_of(head, t + ahead))
+                local_tile(tile_of(head, t + ahead - lead))
             for way in range(2):
                 @pl.when(passes(way, tile))
                 def _():
                     ring_copy(way, head, tile).start()
-            if not local:
+            if relaying:
                 for way in range(2):
                     @pl.when(jnp.logical_and(middle(way), t >= keep))
                     def _():
@@ -285,10 +296,12 @@
             return carry
         return step
 
+    with jax.named_scope("phase1o"):
+        lax.fori_loop(0, lead, produce(False, False), 0)
     with jax.named_scope("phase1a"):
-        lax.fori_loop(0, tiles - ahead, produce(True), 0)
+        lax.fori_loop(lead, tiles - ahead + lead, produce(True, False), 0)
     with jax.named_scope("phase1b"):
-        lax.fori_loop(tiles - ahead, tiles, produce(False), 0)
+        lax.fori_loop(tiles - ahead + lead, tiles, produce(False, True), 0)
 
     def joined(origin, q):
         return jnp.concatenate([gather_ref[origin, 4 * q + i] for i in range(4)], axis=1)
@@ -301,20 +314,22 @@
         rows = pl.ds(pl.multiple_of(i * (4 * TILE), 4 * TILE), 4 * TILE)
         acc_ref[n_head + origin] += dot(joined(origin, i if way == 0 else keep // 4 + i), help_ref[rows, :], 1, 0)
 
-    def share_copy(slot, target):
+    def share_copy(slot, k):
+        target = partner(k)
         return pltpu.make_async_remote_copy(
-            src_ref=share_ref.at[slot, pl.ds(target * rows_per, rows_per), :],
-            dst_ref=shares_ref.at[slot, lax.rem(seq - target + n_seq, n_seq) - 1],
+            src_ref=share_ref.at[slot, pl.ds(pl.multiple_of(target * rows_per, rows_per), rows_per), :],
+            dst_ref=shares_ref.at[slot, k - 1],
             send_sem=share_send.at[slot], recv_sem=share_recv.at[slot],
             device_id=(target, head), device_id_type=MESH,
         )
 
     def send_share(slot):
         share_ref[slot] = (acc_ref[slot] * scale).astype(BF16)
-        for target in range(reducers):
-            @pl.when(seq != target)
-            def _():
-                share_copy(slot, target).start()
+        for k in range(n_seq - 1, 0, -1):
+            if reducers == n_seq:
+                share_copy(slot, k).start()
+            else:
+                pl.when(partner(k) < reducers)(lambda: share_copy(slot, k).start())
 
     def final_copy(slot, block, origin, kind, owner):
         columns = pl.ds(owner * piece if piece < width else 0, piece)
@@ -426,12 +441,13 @@
                 def _():
                     pl.when(place == last)(functools.partial(arrive, way, origin, q))
                     multiply(origin, q)
+                done = jnp.where(place == last, keep // 4 - 1, quads - 1)
+                pl.when(j == done)(functools.partial(send_share, origin))
                 if helps:
                     @pl.when(jnp.logical_and(helper(way), jnp.logical_not(kept_quad(way, q))))
                     def _():
                         multiply_help(way, origin, 0)
                         send_share(n_head + origin)
-                pl.when(j == quads - 1)(functools.partial(send_share, origin))
 
         distance = u // quads
         j = u - quads * distance
@@ -454,8 +470,11 @@
                 def _():
                     @pl.when(distance == 0)
                     def _():
-                        for i in range(spare):
-                            help_copy(way, i).wait_recv()
+                        pltpu.make_async_remote_copy(
+                            src_ref=help_ref, dst_ref=help_ref,
+                            send_sem=help_send.at[0], recv_sem=help_recv.at[0],
+                            device_id=(seq, left if way == 0 else right), device_id_type=MESH,
+                        ).wait_recv()
                     multiply_help(way, origin, 0)
 
         @pl.when(j == quads - 1)
@@ -643,13 +662,13 @@
             dma((1,)),
             dma((1,)),
             dma((2,)),
-            dma((n_head, tiles)),
+            dma((max(1, n_head - 1), tiles)),
             dma((slots,)),
             dma((slots,)),
             dma((slots,)),
             dma((2,)),
             dma((1,)),
-            dma((spare,)),
+            dma((1,)),
         ],
         compiler_params=pltpu.CompilerParams(
             collective_id=0, has_side_effects=True, vmem_limit_bytes=60 * 2**20

time: 48 us -> 46.3 us (0.965)
  Pallas kernels: 47.2 us -> 45.3 us
    pallas_call x1, Pallas kernels: 46.3 us -> 44.4 us  [body(): pl.pallas_call(functools.partial(kernel, n_seq, n_head), out_shape=(pltpu...]
where the time goes in v3:
time: 46.3 us; the launch traced here: 45.9 us
  Pallas kernels  45.3 us (98%)
  between operations  0.64 us (1%)
    pallas_call x1, Pallas kernels, body(): pl.pallas_call(functools.partial(kernel, n_seq, n_head), out_shape=(pltpu...  44.4 us

profile of v3, /device:TPU:7, one launch (start us, length us, event | category | flops | bytes accessed | tf_op | source)
XLA Modules:
  0.0 45.9 jit_solution(11492140514990452024)
XLA Ops:
  0.6 44.4 %shard_map.77 = (bf16[2048,128]{1,0:T(8,128)(2,1)S(1)}, f32[128,256]{1,0:T(8,128)S(1)}) custom-call(bf16[2048,128]{1,0:T(8,128)(2,1)} %q_hbm.1, bf16[2048,128]{1,0:T(8,128)(2,1)} %k_hbm.1, bf16[2048,128]{1,0:T(8,128)(2,1)} %v_hbm.1, s32[1,2048]{1,0:T(1,128)} %bitcast.2, f32[15,64]{1,0:T(8,128)} %bitcast.3, bf16[2048,512]{1,0:T(8,128)(2,1)} %cot_hbm.1), custom_call_target="tpu_custom_call" | custom-call | tf_op jit(solution)/shard_map/pallas_call | solution.py:632
  45.1 0.8 %shard_map.78 = (bf16[2048,128]{1,0:T(8,128)(2,1)}, f32[256,128]{1,0:T(8,128)}) custom-call(bf16[2048,128]{1,0:T(8,128)(2,1)S(1)} %get-tuple-element.4.attn_ref, f32[128,256]{1,0:T(8,128)S(1)} %get-tuple-element.5.grad_ref), custom_call_target="tpu_custom_call" | custom-call | tf_op jit(solution)/shard_map/pallas_call | solution.py:677

commit v4 on v3

--- a/solution.py
+++ b/solution.py
@@ -9,10 +9,10 @@
 
 EPSILON = 1e-06
 TILE = 128
-KEEP = 12
+KEEP = 11
 AHEAD = 8
-LEAD = 4
-LAG = 6
+LEAD = 6
+LAG = 5
 BURST = 2
 MESH = pl.DeviceIdType.MESH
 F32 = jnp.float32
@@ -43,7 +43,7 @@
     attn_ref, grad_ref,
     q_ref, k_ref, v_ref, cot_ref, ids_ref, table_ref, levels_ref, coeff_ref, total_ref, sib_ref,
     state_ref, states_ref, flat_ref, gather_ref, acc_ref,
-    share_ref, shares_ref, final_ref, finals_ref, help_ref,
+    share_ref, shares_ref, final_ref, finals_ref, whole_ref, help_ref,
     load_sem, state_send, state_recv, ring_send, ring_recv,
     share_send, share_recv, final_send, final_recv, help_send, help_recv,
 ):
@@ -188,7 +188,7 @@
         return c >= spare if way == 0 else c < keep
 
     def kept_quad(way, q):
-        return 4 * q >= spare if way == 0 else 4 * q < keep
+        return 4 * q + 3 >= spare if way == 0 else 4 * q < keep
 
     def help_copy(way, i):
         return pltpu.make_async_remote_copy(
@@ -208,6 +208,16 @@
     with jax.named_scope("local1"):
         local_tiles(0, ahead)
     acc_ref[...] = jnp.zeros_like(acc_ref)
+    for way in range(2):
+        blank = range(spare // 4 * 4, spare) if way == 0 else range(keep, (keep + 3) // 4 * 4)
+
+        @pl.when(places[way] == last)
+        def _():
+            for c in blank:
+                for origin in range(n_head):
+                    @pl.when(origin != head)
+                    def _():
+                        gather_ref[origin, c] = jnp.zeros((head_dim, TILE), BF16)
 
     with jax.named_scope("states"):
         for block in range(1, n_seq):
@@ -299,7 +309,7 @@
     with jax.named_scope("phase1o"):
         lax.fori_loop(0, lead, produce(False, False), 0)
     with jax.named_scope("phase1a"):
-        lax.fori_loop(lead, tiles - ahead + lead, produce(True, False), 0)
+        lax.fori_loop(lead, tiles - ahead + lead, produce(True, True), 0)
     with jax.named_scope("phase1b"):
         lax.fori_loop(tiles - ahead + lead, tiles, produce(False, True), 0)
 
@@ -310,9 +320,13 @@
         rows = pl.ds(pl.multiple_of(q * (4 * TILE), 4 * TILE), 4 * TILE)
         acc_ref[origin] += dot(joined(origin, q), cot_ref[rows, :], 1, 0)
 
-    def multiply_help(way, origin, i):
-        rows = pl.ds(pl.multiple_of(i * (4 * TILE), 4 * TILE), 4 * TILE)
-        acc_ref[n_head + origin] += dot(joined(origin, i if way == 0 else keep // 4 + i), help_ref[rows, :], 1, 0)
+    def multiply_help(way, origin):
+        base = 0 if way == 0 else keep
+        for start in range(0, spare, 4):
+            group = range(start, min(start + 4, spare))
+            block = jnp.concatenate([gather_ref[origin, base + i] for i in group], axis=1)
+            rows = help_ref[start * TILE : (group[-1] + 1) * TILE, :]
+            acc_ref[n_head + origin] += dot(block, rows, 1, 0)
 
     def share_copy(slot, k):
         target = partner(k)
@@ -356,7 +370,7 @@
             whole = acc_ref[slot, mine, :] * scale
             for source in range(n_seq - 1):
                 whole += shares_ref[slot, source].astype(F32)
-            final_ref[slot] = whole
+            final_ref[slot] = whole.astype(BF16)
             for owner in range(owners):
                 @pl.when(jnp.logical_not(is_self(block, origin, owner)))
                 def _():
@@ -371,7 +385,9 @@
 
     def arrive(way, origin, q):
         for c in range(4):
-            ring_copy(way, origin, 4 * q + c).wait_recv()
+            @pl.when(kept(way, 4 * q + c))
+            def _():
+                ring_copy(way, origin, 4 * q + c).wait_recv()
 
     def helper(way):
         return jnp.logical_and(places[way] == last - 1, helps)
@@ -441,12 +457,12 @@
                 def _():
                     pl.when(place == last)(functools.partial(arrive, way, origin, q))
                     multiply(origin, q)
-                done = jnp.where(place == last, keep // 4 - 1, quads - 1)
+                done = jnp.where(place == last, (keep + 3) // 4 - 1, quads - 1)
                 pl.when(j == done)(functools.partial(send_share, origin))
                 if helps:
-                    @pl.when(jnp.logical_and(helper(way), jnp.logical_not(kept_quad(way, q))))
+                    @pl.when(jnp.logical_and(helper(way), j == quads - 1))
                     def _():
-                        multiply_help(way, origin, 0)
+                        multiply_help(way, origin)
                         send_share(n_head + origin)
 
         distance = u // quads
@@ -475,7 +491,7 @@
                             send_sem=help_send.at[0], recv_sem=help_recv.at[0],
                             device_id=(seq, left if way == 0 else right), device_id_type=MESH,
                         ).wait_recv()
-                    multiply_help(way, origin, 0)
+                    multiply_help(way, origin)
 
         @pl.when(j == quads - 1)
         def _():
@@ -528,18 +544,19 @@
                         send_sem=final_send.at[0], recv_sem=final_recv.at[kind],
                         device_id=(0, plane), device_id_type=MESH,
                     ).wait_recv()
+        whole_ref[...] = finals_ref[0].astype(F32)
         if helps:
             @pl.when(at_end)
             def _():
-                finals_ref[0] += finals_ref[1]
+                whole_ref[...] += finals_ref[1].astype(F32)
         per = grad_ref.shape[1]
         if per == piece:
-            grad_ref[...] = finals_ref[0]
+            grad_ref[...] = whole_ref[...]
         else:
             for owner in range(owners):
                 @pl.when(lax.rem(seq, owners) == owner)
                 def _():
-                    grad_ref[...] = finals_ref[0][:, owner * per : (owner + 1) * per]
+                    grad_ref[...] = whole_ref[:, owner * per : (owner + 1) * per]
 
     with jax.named_scope("drain"):
         for block in range(n_seq - 1):
@@ -655,8 +672,9 @@
             pltpu.VMEM((slots, head_dim, width), F32),
             pltpu.VMEM((slots, head_dim, width), BF16),
             pltpu.VMEM((slots, n_seq - 1, rows_per, width), BF16),
-            pltpu.VMEM((slots, rows_per, width), F32),
-            pltpu.VMEM((2, head_dim, piece), F32),
+            pltpu.VMEM((slots, rows_per, width), BF16),
+            pltpu.VMEM((2, head_dim, piece), BF16),
+            pltpu.VMEM((head_dim, piece), F32),
             pltpu.VMEM((spare * TILE, width), BF16),
             dma((6,)),
             dma((1,)),

time: 46.3 us -> 45.3 us (0.978)
  Pallas kernels: 45.3 us -> 43.9 us
    pallas_call x1, Pallas kernels: 44.4 us -> 43.1 us  [body(): pl.pallas_call(functools.partial(kernel, n_seq, n_head), out_shape=(pltpu...]
where the time goes in v4:
time: 45.3 us; the launch traced here: 44.5 us
  Pallas kernels  43.9 us (97%)
  between operations  0.64 us (1%)
    pallas_call x1, Pallas kernels, body(): pl.pallas_call(functools.partial(kernel, n_seq, n_head), out_shape=(pltpu...  43.1 us

profile of v4, /device:TPU:7, one launch (start us, length us, event | category | flops | bytes accessed | tf_op | source)
XLA Modules:
  0.0 44.5 jit_solution(8614647378084792779)
XLA Ops:
  0.6 43.1 %shard_map.77 = (bf16[2048,128]{1,0:T(8,128)(2,1)S(1)}, f32[128,256]{1,0:T(8,128)S(1)}) custom-call(bf16[2048,128]{1,0:T(8,128)(2,1)} %q_hbm.1, bf16[2048,128]{1,0:T(8,128)(2,1)} %k_hbm.1, bf16[2048,128]{1,0:T(8,128)(2,1)} %v_hbm.1, s32[1,2048]{1,0:T(1,128)} %bitcast.2, f32[15,64]{1,0:T(8,128)} %bitcast.3, bf16[2048,512]{1,0:T(8,128)(2,1)} %cot_hbm.1), custom_call_target="tpu_custom_call" | custom-call | tf_op jit(solution)/shard_map/pallas_call | solution.py:649
  43.7 0.8 %shard_map.78 = (bf16[2048,128]{1,0:T(8,128)(2,1)}, f32[256,128]{1,0:T(8,128)}) custom-call(bf16[2048,128]{1,0:T(8,128)(2,1)S(1)} %get-tuple-element.4.attn_ref, f32[128,256]{1,0:T(8,128)S(1)} %get-tuple-element.5.grad_ref), custom_call_target="tpu_custom_call" | custom-call | tf_op jit(solution)/shard_map/pallas_call | solution.py:695

commit v5 on v4

--- a/solution.py
+++ b/solution.py
@@ -12,7 +12,8 @@
 KEEP = 11
 AHEAD = 8
 LEAD = 6
-LAG = 5
+LAG = 6
+SETTLED = 12
 BURST = 2
 MESH = pl.DeviceIdType.MESH
 F32 = jnp.float32
@@ -91,6 +92,54 @@
     pl.when(head < n_head - 1)(lambda: greet((seq, head + 1)))
 
     levels_ref[...] = tile_levels(TILE)
+    right, left = lax.rem(head + 1, n_head), lax.rem(head + n_head - 1, n_head)
+    neighbours = (right, left)
+    places = (head, last - head)
+
+    half = n_head // 2
+    spare = tiles - keep
+
+    def origin_of(way, distance):
+        return head - distance if way == 0 else head + distance
+
+    def upward(origin):
+        inside = jnp.logical_and(origin > 0, origin < half)
+        return jnp.logical_or(inside, origin == last)
+
+    def tile_of(origin, i):
+        return jnp.where(upward(origin), i, tiles - 1 - i)
+
+    def quad_of(origin, j):
+        return jnp.where(upward(origin), j, quads - 1 - j)
+
+    def kept(way, c):
+        return c >= spare if way == 0 else c < keep
+
+    def kept_quad(way, q):
+        return 4 * q + 3 >= spare if way == 0 else 4 * q < keep
+
+    def help_copy(way, i):
+        return pltpu.make_async_remote_copy(
+            src_ref=cot_hbm.at[pl.ds(i * TILE if way == 0 else (keep + i) * TILE, TILE), :],
+            dst_ref=help_ref.at[pl.ds(i * TILE, TILE), :],
+            send_sem=help_send.at[0], recv_sem=help_recv.at[0],
+            device_id=(seq, left if way == 0 else right), device_id_type=MESH,
+        )
+
+    at_edge = jnp.logical_or(head == 0, head == last)
+
+    def meet():
+        pl.semaphore_wait(barrier, n_seq - 1 + jnp.minimum(head, 1) + jnp.minimum(last - head, 1))
+
+    @pl.when(at_edge)
+    def _():
+        meet()
+        for way in range(2):
+            @pl.when(places[way] == last)
+            def _():
+                for i in range(spare):
+                    help_copy(way, i).start()
+
     with jax.named_scope("kv"):
         for load in loads[:4]:
             load.wait()
@@ -143,7 +192,7 @@
         lax.fori_loop(start, stop, one, 0, unroll=True)
 
     with jax.named_scope("barrier"):
-        pl.semaphore_wait(barrier, n_seq - 1 + jnp.minimum(head, 1) + jnp.minimum(last - head, 1))
+        pl.when(jnp.logical_not(at_edge))(meet)
 
     def state_copy(target):
         return pltpu.make_async_remote_copy(
@@ -163,46 +212,6 @@
         @pl.when(seq < partner(k))
         def _():
             state_copy(partner(k)).start()
-
-    right, left = lax.rem(head + 1, n_head), lax.rem(head + n_head - 1, n_head)
-    neighbours = (right, left)
-    places = (head, last - head)
-
-    half = n_head // 2
-    spare = tiles - keep
-
-    def origin_of(way, distance):
-        return head - distance if way == 0 else head + distance
-
-    def upward(origin):
-        inside = jnp.logical_and(origin > 0, origin < half)
-        return jnp.logical_or(inside, origin == last)
-
-    def tile_of(origin, i):
-        return jnp.where(upward(origin), i, tiles - 1 - i)
-
-    def quad_of(origin, j):
-        return jnp.where(upward(origin), j, quads - 1 - j)
-
-    def kept(way, c):
-        return c >= spare if way == 0 else c < keep
-
-    def kept_quad(way, q):
-        return 4 * q + 3 >= spare if way == 0 else 4 * q < keep
-
-    def help_copy(way, i):
-        return pltpu.make_async_remote_copy(
-            src_ref=cot_hbm.at[pl.ds(i * TILE if way == 0 else (keep + i) * TILE, TILE), :],
-            dst_ref=help_ref.at[pl.ds(i * TILE, TILE), :],
-            send_sem=help_send.at[0], recv_sem=help_recv.at[0],
-            device_id=(seq, left if way == 0 else right), device_id_type=MESH,
-        )
-
-    for way in range(2):
-        @pl.when(places[way] == last)
-        def _():
-            for i in range(spare):
-                help_copy(way, i).start()
 
     loads[4].wait()
     with jax.named_scope("local1"):
@@ -496,11 +505,16 @@
         @pl.when(j == quads - 1)
         def _():
             every_group(distance, lambda slot, *_: send_share(slot))
-            pl.when(jnp.logical_and(farthest == last, distance >= 2))(lambda: every_group(distance - 2, reduce_share))
+
+        behind = jnp.maximum(u - SETTLED, 0)
+
+        @pl.when(jnp.logical_and(jnp.logical_and(u >= SETTLED, lax.rem(behind, quads) == 0), behind // quads < farthest))
+        def _():
+            every_group(behind // quads, reduce_share)
         return carry
 
     with jax.named_scope("flow"):
-        lax.fori_loop(0, jnp.maximum(tiles + 1 + LAG * (farthest - 1), quads * (farthest + 2)), flow, 0)
+        lax.fori_loop(0, jnp.maximum(tiles + 1 + LAG * (farthest - 1), quads * (farthest - 1) + SETTLED + 1), flow, 0)
 
     ends = []
     for way in range(2):
@@ -511,14 +525,6 @@
         place, origin = places[way], block_of(1 - way)
         ends.append((place > 0, origin, head, origin, 0))
     with jax.named_scope("reducelast"):
-        @pl.when(farthest < last)
-        def _():
-            def one(distance, carry):
-                every_group(distance, reduce_share)
-                return carry
-
-            lax.fori_loop(0, farthest, one, 0)
-
         for condition, *rest in ends[:-2]:
             pl.when(condition)(functools.partial(reduce_share, *rest))
         closer = places[0] <= places[1]

time: 45.3 us -> 45 us (level)
  no operation moved by 1% of the time
where the time goes in v5:
time: 45 us; the launch traced here: 44.5 us
  Pallas kernels  43.8 us (97%)
  between operations  0.64 us (1%)
    pallas_call x1, Pallas kernels, body(): pl.pallas_call(functools.partial(kernel, n_seq, n_head), out_shape=(pltpu...  43 us

profile of v5, /device:TPU:7, one launch (start us, length us, event | category | flops | bytes accessed | tf_op | source)
XLA Modules:
  0.0 44.5 jit_solution(13055984560674133304)
XLA Ops:
  0.6 43.0 %shard_map.77 = (bf16[2048,128]{1,0:T(8,128)(2,1)S(1)}, f32[128,256]{1,0:T(8,128)S(1)}) custom-call(bf16[2048,128]{1,0:T(8,128)(2,1)} %q_hbm.1, bf16[2048,128]{1,0:T(8,128)(2,1)} %k_hbm.1, bf16[2048,128]{1,0:T(8,128)(2,1)} %v_hbm.1, s32[1,2048]{1,0:T(1,128)} %bitcast.2, f32[15,64]{1,0:T(8,128)} %bitcast.3, bf16[2048,512]{1,0:T(8,128)(2,1)} %cot_hbm.1), custom_call_target="tpu_custom_call" | custom-call | tf_op jit(solution)/shard_map/pallas_call | solution.py:655
  43.6 0.8 %shard_map.78 = (bf16[2048,128]{1,0:T(8,128)(2,1)}, f32[256,128]{1,0:T(8,128)}) custom-call(bf16[2048,128]{1,0:T(8,128)(2,1)S(1)} %get-tuple-element.4.attn_ref, f32[128,256]{1,0:T(8,128)S(1)} %get-tuple-element.5.grad_ref), custom_call_target="tpu_custom_call" | custom-call | tf_op jit(solution)/shard_map/pallas_call | solution.py:701

commit v6 on v5

--- a/solution.py
+++ b/solution.py
@@ -525,14 +525,17 @@
         place, origin = places[way], block_of(1 - way)
         ends.append((place > 0, origin, head, origin, 0))
     with jax.named_scope("reducelast"):
+        closer = places[0] <= places[1]
+        nearer = (closer, jnp.logical_not(closer))
+
+        def reduce_main(flip):
+            for turn, (condition, *rest) in zip(flip, ends[-2:]):
+                pl.when(jnp.logical_and(turn, condition))(functools.partial(reduce_share, *rest))
+
+        reduce_main(nearer)
         for condition, *rest in ends[:-2]:
             pl.when(condition)(functools.partial(reduce_share, *rest))
-        closer = places[0] <= places[1]
-        for flip, pair in ((closer, ends[-2:]), (jnp.logical_not(closer), ends[-2:][::-1])):
-            @pl.when(flip)
-            def _():
-                for condition, *rest in pair:
-                    pl.when(condition)(functools.partial(reduce_share, *rest))
+        reduce_main(nearer[::-1])
 
     with jax.named_scope("finals"):
         home = seq // owners

time: 45 us -> 45 us (level)
  no operation moved by 1% of the time
where the time goes in v6:
time: 45 us; the launch traced here: 44.8 us
  Pallas kernels  44.2 us (98%)
  between operations  0.64 us (1%)
    pallas_call x1, Pallas kernels, body(): pl.pallas_call(functools.partial(kernel, n_seq, n_head), out_shape=(pltpu...  43.3 us

profile of v6, /device:TPU:7, one launch (start us, length us, event | category | flops | bytes accessed | tf_op | source)
XLA Modules:
  0.0 44.8 jit_solution(17023402559481097755)
XLA Ops:
  0.6 43.3 %shard_map.77 = (bf16[2048,128]{1,0:T(8,128)(2,1)S(1)}, f32[128,256]{1,0:T(8,128)S(1)}) custom-call(bf16[2048,128]{1,0:T(8,128)(2,1)} %q_hbm.1, bf16[2048,128]{1,0:T(8,128)(2,1)} %k_hbm.1, bf16[2048,128]{1,0:T(8,128)(2,1)} %v_hbm.1, s32[1,2048]{1,0:T(1,128)} %bitcast.2, f32[15,64]{1,0:T(8,128)} %bitcast.3, bf16[2048,512]{1,0:T(8,128)(2,1)} %cot_hbm.1), custom_call_target="tpu_custom_call" | custom-call | tf_op jit(solution)/shard_map/pallas_call | solution.py:658
  44.0 0.8 %shard_map.78 = (bf16[2048,128]{1,0:T(8,128)(2,1)}, f32[256,128]{1,0:T(8,128)}) custom-call(bf16[2048,128]{1,0:T(8,128)(2,1)S(1)} %get-tuple-element.4.attn_ref, f32[128,256]{1,0:T(8,128)S(1)} %get-tuple-element.5.grad_ref), custom_call_target="tpu_custom_call" | custom-call | tf_op jit(solution)/shard_map/pallas_call | solution.py:704
